TPU v7x, 512 devices: a whole 4x8x8 slice. The times are simulated.
512 devices in a mesh: row: 32 (over y, x), col: 2 (over core), depth: 8 (over z).
Axes of the slice: x: 4, y: 8, z: 8, core: 2. Of those that a mesh axis runs over, the one named last changes fastest.
Arguments:
- trailing: float32 [16384, 16384], P('row', ('col', 'depth')), may hold values from -6 to 778, as said below
- panel_parts: float32 [8, 16384, 256], P('depth', 'row', 'col')
- diag_parts: float32 [8, 256, 256], P('depth'), as said below
Outputs:
- updated: float32 [16384, 16384], P('row', ('col', 'depth'))
- first_factor: float32 [16384, 256], P('row', 'col')
- second_factor: float32 [16384, 256], P('row', 'col')
Inputs may be any that keep to these rules, and one draw needn't show every extreme that they name: The matrix with diagonal tile (sum of diag_parts), block column (sum of panel_parts) and trailing block A, in global order, is symmetric positive definite, and so is the trailing block after the first block column is eliminated. `diag_parts`: each layer's tile is symmetric.
All inputs are finite; a program needn't handle non-finite values.
Results may differ from a plain program's by a relative error of at most 0.000084.
Values sent between devices are 32-bit elements; how exact they have to be, the bound alone decides.
A program may use at most 128 MiB of HBM per device.

v0:
```python
import jax
import jax.numpy as jnp
from jax import lax
from jax.sharding import Mesh
from jax.sharding import PartitionSpec as P

ROW = ("row_0", "row_1")
ROW_COL_DEPTH = ("row_0", "row_1", "col", "depth")


def from_root(shard, axis, root):
    return lax.dynamic_index_in_dim(lax.all_gather(shard, axis), root, 0, keepdims=False)


def spread(shard, axes, root):
    shard = jnp.where(lax.axis_index(axes) == root, shard, jnp.zeros_like(shard))
    for axis in axes:
        shard = lax.psum(shard, axis)
    return shard


def spread_2(shard, axis, root):
    mine = lax.axis_index(axis) == root
    return lax.psum(jnp.where(mine, shard, jnp.zeros_like(shard)), axis)


def solve_right(factor, block):
    return jax.scipy.linalg.solve_triangular(factor, block.T, lower=True).T


def on_device(trailing, panel_parts, diag_parts):
    rows_dev, cols_dev = trailing.shape
    tile_size = diag_parts.shape[1]
    width_col = panel_parts.shape[2]
    tiles_col = cols_dev // tile_size
    n_row = lax.axis_size(ROW)
    n_col = lax.axis_size("col")
    my_row = lax.axis_index(ROW)
    my_col = lax.axis_index("col")
    my_depth = lax.axis_index("depth")

    def owner_of(column_tile):
        global_tile = (my_depth * tiles_col + column_tile) * n_col + my_col
        return (global_tile % n_row, global_tile // n_row)

    initial = from_root(trailing[:, :tile_size], ("col", "depth"), 0)
    corner_start = spread(trailing[:tile_size, :tile_size], ROW_COL_DEPTH, 0)
    local_panel = panel_parts[0]
    local_diag = diag_parts[0]
    summed, diagonal = lax.psum((local_panel, local_diag), "depth")
    panel_full = lax.all_gather(summed, "col", axis=1, tiled=True)
    lead_factor = jnp.linalg.cholesky(diagonal)
    first_factor = solve_right(lead_factor, panel_full)
    first_pieces = []
    for column_tile in range(tiles_col):
        owner_row, local_tile = owner_of(column_tile)
        slab_piece = lax.dynamic_slice_in_dim(first_factor, local_tile * tile_size, tile_size, 0)
        first_pieces.append(spread_2(slab_piece, ROW, owner_row))
    across = jnp.concatenate(first_pieces, axis=0)
    updated_once = trailing - jnp.dot(first_factor, across.T, precision=lax.Precision.HIGHEST)
    leading_rows = from_root(first_factor[:tile_size], ROW, 0)
    column = initial - jnp.dot(first_factor, leading_rows.T, precision=lax.Precision.HIGHEST)
    corner = corner_start - jnp.dot(leading_rows, leading_rows.T, precision=lax.Precision.HIGHEST)
    next_factor = jnp.linalg.cholesky(corner)
    second_factor = solve_right(next_factor, column)
    row_numbers = jnp.arange(rows_dev, dtype=jnp.int32)
    keep_rows = jnp.where((my_row == 0) & (row_numbers < tile_size), 0.0, 1.0).astype(jnp.float32)
    masked = second_factor * keep_rows[:, None]
    second_pieces = []
    for column_tile in range(tiles_col):
        owner_row, local_tile = owner_of(column_tile)
        slab_piece = lax.dynamic_slice_in_dim(masked, local_tile * tile_size, tile_size, 0)
        second_pieces.append(spread_2(slab_piece, ROW, owner_row))
    across_second = jnp.concatenate(second_pieces, axis=0)
    updated = updated_once - jnp.dot(masked, across_second.T, precision=lax.Precision.HIGHEST)
    first_share = lax.dynamic_slice_in_dim(first_factor, my_col * width_col, width_col, 1)
    second_share = lax.dynamic_slice_in_dim(second_factor, my_col * width_col, width_col, 1)
    return (updated, first_share, second_share)


def solution(mesh):
    finer = Mesh(
        mesh.devices.reshape(8, 4, mesh.shape["col"], mesh.shape["depth"]),
        ("row_0", "row_1", "col", "depth"),
    )
    return jax.shard_map(
        on_device,
        mesh=finer,
        in_specs=(P(ROW, ("col", "depth")), P("depth", ROW, "col"), P("depth", None, None)),
        out_specs=(P(ROW, ("col", "depth")), P(ROW, "col"), P(ROW, "col")),
        check_vma=False,
    )
```

profile of v0, /device:TPU:64, one launch (start us, length us, event | category | flops | bytes accessed | tf_op | source)
XLA Modules:
  0.0 684.5 jit_solution(6929470779380657949)
XLA Ops:
  9.2 83.7 %all-reduce.9.cloned.1.call-done = f32[256,256]{0,1:T(8,128)} async-done(((f32[256,256]{0,1:T(8,128)}), f32[256,256]{0,1:T(8,128)}) %all-reduce.9.cloned.1.call-update) | async-done | bytes 262160 | tf_op jit(solution)/shard_map/psum | solution.py:18
  93.0 53.5 %all-reduce.11.cloned.1.call-done = f32[256,256]{0,1:T(8,128)} async-done(((f32[256,256]{0,1:T(8,128)}), f32[256,256]{0,1:T(8,128)}) %all-reduce.11.cloned.1.call-update) | async-done | bytes 262160 | tf_op jit(solution)/shard_map/psum | solution.py:18
  147.5 37.2 %all-reduce.13.cloned.1.call-done = f32[256,256]{0,1:T(8,128)} async-done(((f32[256,256]{0,1:T(8,128)}), f32[256,256]{0,1:T(8,128)}) %all-reduce.13.cloned.1.call-update) | async-done | bytes 262160 | tf_op jit(solution)/shard_map/psum | solution.py:18
  184.7 85.0 %all-reduce.17.cloned.1.call-done = (f32[512,128]{1,0:T(8,128)}, f32[256,256]{0,1:T(8,128)}, f32[256,256]{0,1:T(8,128)}) async-done(((f32[512,128]{1,0:T(8,128)}, f32[256,256]{0,1:T(8,128)}, f32[256,256]{0,1:T(8,128)}), (f32[512,128]{1,0:T(8,128)}, f32[256,256]{0,1:T(8,128)}, f32[256,256]{0,1:T(8,128)})) %all-reduce.17.cloned.1.call-update) | async-done | bytes 786448 | tf_op jit(solution)/shard_map/psum | solution.py:50
  271.9 11.7 %cholesky.130 = f32[128,128]{1,0:T(8,128)S(1)} custom-call(f32[128,128]{1,0:T(8,128)S(1)} %cholesky.194), custom_call_target="Cholesky" | custom-call | tf_op jit(solution)/shard_map/jit(cholesky)/cholesky | solution.py:52
  283.6 9.8 %custom-call.13 = f32[1,128,128]{1,2,0:T(8,128)S(1)} custom-call(f32[1,128,128]{2,1,0:T(8,128)S(1)} %get-tuple-element.67), custom_call_target="InvertDiagBlocksLowerTriangular" | custom-call | tf_op jit(solution)/shard_map/jit(cholesky)/cholesky | solution.py:52
  294.0 11.7 %cholesky.147 = f32[128,128]{1,0:T(8,128)S(1)} custom-call(f32[128,128]{1,0:T(8,128)S(1)} %convolution_subtract_fusion.5), custom_call_target="Cholesky" | custom-call | tf_op jit(solution)/shard_map/jit(cholesky)/cholesky | solution.py:52
  307.8 4.2 while.4
  308.6 1.4 bitcast_dynamic-update-slice_fusion.4
  310.6 1.4 bitcast_dynamic-update-slice_fusion.4
  312.0 19.7 %custom-call.14 = f32[2,128,128]{1,2,0:T(8,128)S(1)} custom-call(f32[2,128,128]{2,1,0:T(8,128)S(1)} %get-tuple-element.19), custom_call_target="InvertDiagBlocksLowerTriangular" | custom-call | tf_op jit(solution)/shard_map/jit(_solve_triangular)/triangular_solve | solution.py:28
  331.7 2.2 all_gather.15
  338.2 99.5 %all-gather.5.cloned.1.call-done = f32[8192,256]{1,0:T(8,128)} async-done(((f32[256,256]{1,0:T(8,128)}), f32[8192,256]{1,0:T(8,128)}) %all-gather.5.cloned.1.call-update) | async-done | bytes 8388624 | tf_op jit(solution)/shard_map/all_gather | solution.py:12
  437.7 1.4 convolution_subtract_fusion.2
  439.4 11.7 %cholesky.164 = f32[128,128]{1,0:T(8,128)S(1)} custom-call(f32[128,128]{1,0:T(8,128)S(1)} %cholesky.197), custom_call_target="Cholesky" | custom-call | tf_op jit(solution)/shard_map/jit(cholesky)/cholesky | solution.py:64
  451.1 9.8 %custom-call.15 = f32[1,128,128]{1,2,0:T(8,128)S(1)} custom-call(f32[1,128,128]{2,1,0:T(8,128)S(1)} %get-tuple-element.63), custom_call_target="InvertDiagBlocksLowerTriangular" | custom-call | tf_op jit(solution)/shard_map/jit(cholesky)/cholesky | solution.py:64
  461.4 11.7 %cholesky.181 = f32[128,128]{1,0:T(8,128)S(1)} custom-call(f32[128,128]{1,0:T(8,128)S(1)} %convolution_subtract_fusion.4), custom_call_target="Cholesky" | custom-call | tf_op jit(solution)/shard_map/jit(cholesky)/cholesky | solution.py:64
  475.8 4.2 while.5
  476.7 1.4 bitcast_dynamic-update-slice_fusion.5
  480.0 19.7 %custom-call.16 = f32[2,128,128]{1,2,0:T(8,128)S(1)} custom-call(f32[2,128,128]{2,1,0:T(8,128)S(1)} %get-tuple-element.20), custom_call_target="InvertDiagBlocksLowerTriangular" | custom-call | tf_op jit(solution)/shard_map/jit(_solve_triangular)/triangular_solve | solution.py:28
  499.7 1.7 fusion
  508.0 163.1 %all-reduce.15.cloned.1.call-done = (f32[256,256]{1,0:T(8,128)}, f32[256,256]{1,0:T(8,128)}, f32[256,256]{1,0:T(8,128)}, f32[256,256]{1,0:T(8,128)}, f32[256,256...) async-done(((f32[256,256]{1,0:T(8,128)}, f32[256,256]{1,0:T(8,128)}, f32[256,256]{1,0:T(8,128)}, f32[256,256]{1,0:T(8,128)}, ...) | async-done | bytes 2097168 | tf_op jit(solution)/shard_map/psum | solution.py:24
  671.1 3.1 fusion.1
  674.3 3.4 subtract_subtract_fusion
  (88 shorter events, 23.0 us)
Async XLA Ops:
  7.2 139.4 %copy-start.8 = (f32[1,256,256]{2,1,0:T(8,128)S(1)}, f32[1,256,256]{2,1,0:T(8,128)}, u32[]{:S(2)}) copy-start(f32[1,256,256]{2,1,0:T(8,128)} %param.8) | copy-start | bytes 786436
  7.2 85.8 %all-reduce.9.cloned.1.call-start = ((), (), s32[]{:S(2)}) async-start(), calls=%async_computation | async-start | bytes 524288 | tf_op jit(solution)/shard_map/psum | solution.py:18
  9.1 137.4 %all-reduce.11.cloned.1.call-start = ((), (), s32[]{:S(2)}) async-start(), calls=%async_computation.1 | async-start | bytes 524288 | tf_op jit(solution)/shard_map/psum | solution.py:18
  93.0 91.7 %all-reduce.13.cloned.1.call-start = ((), (), s32[]{:S(2)}) async-start(), calls=%async_computation.2 | async-start | bytes 524288 | tf_op jit(solution)/shard_map/psum | solution.py:18
  146.6 123.2 %all-reduce.17.cloned.1.call-start = ((), (), s32[]{:S(2)}) async-start(), calls=%async_computation.6 | async-start | bytes 1572864 | tf_op jit(solution)/shard_map/psum | solution.py:50
  184.7 253.1 %all-gather.5.cloned.1.call-start = ((), (), s32[]{:S(2)}) async-start(), calls=%async_computation.3 | async-start | bytes 8650752 | tf_op jit(solution)/shard_map/all_gather | solution.py:12
  269.7 61.9 %copy-start.3 = (f32[512,128]{1,0:T(8,128)S(1)}, f32[512,128]{1,0:T(8,128)}, u32[]{:S(2)}) copy-start(f32[512,128]{1,0:T(8,128)} %get-tuple-element.45) | copy-start | bytes 786436
  333.8 2.4 copy-start
  335.4 102.3 %copy-start.2 = (f32[256,256]{0,1:T(8,128)S(1)}, f32[256,256]{0,1:T(8,128)}, u32[]{:S(2)}) copy-start(f32[256,256]{0,1:T(8,128)} %get-tuple-element.47) | copy-start | bytes 786436
  336.2 163.6 %all-gather.7.cloned.1.call-start = ((), (), s32[]{:S(2)}) async-start(), calls=%async_computation.4 | async-start | bytes 8912896 | tf_op jit(solution)/shard_map/all_gather | solution.py:12
  337.1 334.0 %all-reduce.15.cloned.1.call-start = ((), (), s32[]{:S(2)}) async-start(), calls=%async_computation.5 | async-start | bytes 4194304 | tf_op jit(solution)/shard_map/psum | solution.py:24
  504.7 0.7 copy-start.1
  671.1 3.2 copy-start.4
  671.1 3.2 copy-start.5
  671.1 3.2 copy-start.6
  671.1 3.2 copy-start.7
Sparse Core Ops, SparseCore 0:
  10.9 82.0 all-reduce.8
  95.3 51.2 all-reduce.10
  149.4 35.1 all-reduce.12
  187.6 82.0 all-reduce.16
  336.3 101.3 all-gather.4
  440.3 54.8 all-gather.6
  506.6 164.4 all-reduce.14
where the time goes:
time: 685 us
  waiting for transfers between devices  522 us (76%)
  other arithmetic  113 us (16%)
  between operations  17.2 us (3%)
  matrix products  15.1 us (2%)
  local copies, waits for them, and re-layouts  13.7 us (2%)
    psum x3, waiting for transfers between devices, spread(): shard = lax.psum(shard, axis)  174 us
    psum x1, waiting for transfers between devices, spread_2(): return lax.psum(jnp.where(mine, shard, jnp.zeros_like(shard)), axis)  163 us
    all_gather x2, waiting for transfers between devices, from_root(): lax.all_gather(shard, axis)  99.5 us
    psum x1, waiting for transfers between devices, on_device(): summed, diagonal = lax.psum((local_panel, local_diag), 'depth')  85 us
    another operation x5, other arithmetic, solve_right(): return jax.scipy.linalg.solve_triangular(factor, block.T, lower=True).T  39.4 us
    another operation x7, other arithmetic, on_device(): next_factor = jnp.linalg.cholesky(corner)  34.6 us
    another operation x6, other arithmetic, on_device(): lead_factor = jnp.linalg.cholesky(diagonal)  34 us
  transfers between devices with their start and end apart: 7, of which 6 were waited for; matrix products, arithmetic and copies ran while one was open for 9% of the time, Pallas kernels for 0%

commit v1 on v0

v1 whole, which is shorter than its diff:
```python
import functools
import jax
import jax.numpy as jnp
from jax import lax
from jax.experimental import pallas as pl
from jax.experimental.pallas import tpu as pltpu
from jax.sharding import PartitionSpec as P

f32, bf16 = jnp.float32, jnp.bfloat16
MESH = pl.DeviceIdType.MESH
NB = 32
NX, NY, NZ = 4, 8, 8
NCH = 2
ORDER_Z = (4, 3, 5, 2, 6, 1, 7)


def split2(v):
    h = v.astype(bf16)
    return h, (v - h.astype(f32)).astype(bf16)


def split3(v):
    h = v.astype(bf16)
    rest = v - h.astype(f32)
    m = rest.astype(bf16)
    return h, m, (rest - m.astype(f32)).astype(bf16)


def dot_bf(a, b, dims):
    return lax.dot_general(a, b, (dims, ((), ())), preferred_element_type=f32)


NT = ((1,), (1,))


def mul_nt(a, b):
    ah, am = a
    bh, bm = b
    return dot_bf(ah, bh, NT) + (dot_bf(ah, bm, NT) + dot_bf(am, bh, NT))


def mul_nt6(a, b):
    ah, am, al = split3(a)
    bh, bm, bl = split3(b)
    low = dot_bf(am, bm, NT) + dot_bf(ah, bl, NT) + dot_bf(al, bh, NT)
    return dot_bf(ah, bh, NT) + (dot_bf(ah, bm, NT) + dot_bf(am, bh, NT) + low)


def bc_row(v, i):
    return jnp.broadcast_to(v[i : i + 1, :], (8, 128))


def factor_block(s_ref, y_ref, first):
    groups = NB // 8
    row0 = pl.multiple_of(first, NB)
    lane0 = pl.multiple_of((first // 128) * 128, 128)
    off = first % 128
    rows = [[s_ref[pl.ds(row0 + 8 * g, 8), 128 * q : 128 * (q + 1)] for q in range(4)] for g in range(groups)]
    diag = [s_ref[pl.ds(row0 + 8 * g, 8), pl.ds(lane0, 128)] for g in range(groups)]
    sub = lax.broadcasted_iota(jnp.int32, (8, 128), 0)
    cols = []
    for j in range(NB):
        idx = jnp.full((8, 128), off + j, jnp.int32)
        cols.append(
            [
                jnp.take_along_axis(diag[g], idx, axis=1, mode="promise_in_bounds") if g >= j // 8 else None
                for g in range(groups)
            ]
        )
    scale = [jnp.ones((8, 128), f32) for _ in range(groups)]
    for j in range(NB):
        gj, rj = divmod(j, 8)
        root = lax.rsqrt(bc_row(cols[j][gj], rj))
        inv = root * root
        mult = [None] * groups
        for g in range(gj, groups):
            mult[g] = cols[j][g] * inv
        for k in range(j + 1, NB):
            gk, rk = divmod(k, 8)
            b = bc_row(cols[j][gk], rk)
            for g in range(gk, groups):
                cols[k][g] = cols[k][g] - mult[g] * b
        scale[gj] = jnp.where(sub == rj, root, scale[gj])
        if rj < 7:
            mult[gj] = jnp.where(sub > rj, mult[gj], 0.0)
        for q in range(4):
            pivot = bc_row(rows[gj][q], rj)
            for g in range(gj if rj < 7 else gj + 1, groups):
                rows[g][q] = rows[g][q] - mult[g] * pivot
    for g in range(groups):
        for q in range(4):
            y_ref[pl.ds(row0 + 8 * g, 8), 128 * q : 128 * (q + 1)] = rows[g][q] * scale[g]


def chol_inverse(s_ref, y_ref):
    i0 = lax.broadcasted_iota(jnp.int32, (256, 256), 0)
    i1 = lax.broadcasted_iota(jnp.int32, (256, 256), 1)
    s_ref[:, 256:] = jnp.where(i0 == i1, 1.0, 0.0).astype(f32)

    def body(b, carry):
        first = b * NB
        factor_block(s_ref, y_ref, first)
        h, m, l = split3(y_ref[pl.ds(pl.multiple_of(first, NB), NB), :])
        left = jnp.concatenate([h, h, m, h, m, l], axis=0)[:, :256]
        right = jnp.concatenate([h, m, h, l, m, h], axis=0)
        s_ref[...] -= dot_bf(left, right, ((0,), (0,)))
        return carry

    lax.fori_loop(0, 256 // NB, body, 0)


def comm_kernel(trail, panel, diag, d_ref, pr, cr, px, cx, pc0, rs_d, rs_p, s_rs, r_rs, s_ag, r_ag, s_c, r_c, s_x, r_x,
                s_q, r_q, s_qx, s_y, r_y, s_t, r_t):
    row, c, z = lax.axis_index("row"), lax.axis_index("col"), lax.axis_index("depth")
    x, y = lax.rem(row, NX), lax.div(row, NX)
    other = (row, 1 - c, z)
    zdev = lambda o: (row, c, lax.rem(z + o, NZ))
    xdev = lambda s: (y * NX + lax.rem(x + s + NX, NX), c, z)
    ydev = lambda s: (lax.rem(y + s + NY, NY) * NX + x, c, z)

    barrier = pltpu.get_barrier_semaphore()
    peers = [zdev(o) for o in range(1, NZ)] + [other, xdev(1), xdev(-1), ydev(1), ydev(-1)]
    for peer in peers:
        pl.semaphore_signal(barrier, inc=1, device_id=peer, device_id_type=MESH)
    pl.semaphore_wait(barrier, len(peers))

    pending = []

    def copy(src, dst, ssem, rsem, dev):
        return pltpu.make_async_remote_copy(src_ref=src, dst_ref=dst, send_sem=ssem, recv_sem=rsem, device_id=dev,
                                            device_id_type=MESH)

    def when(cond, fn):
        if cond is None:
            fn()
        else:
            pl.when(cond)(fn)

    def send(make, cond=None):
        when(cond, lambda: make().start())
        pending.append((make, cond))

    def recv(dst, ssem, rsem, cond=None):
        when(cond, lambda: copy(dst, dst, ssem, rsem, other).wait_recv())

    for o in ORDER_Z:
        send(lambda o=o: copy(diag.at[lax.rem(z + o, NZ), c], rs_d.at[o - 1], s_rs.at[0, o - 1], r_rs.at[0, o - 1], zdev(o)))
    for o in ORDER_Z:
        send(lambda o=o: copy(panel.at[lax.rem(z + o, NZ)], rs_p.at[o - 1], s_rs.at[1, o - 1], r_rs.at[1, o - 1], zdev(o)))
    source = (c == 0) & (z == 0)
    for o in ORDER_Z:
        send(lambda o=o: copy(trail.at[64 * o : 64 * (o + 1), 0:256], cr.at[o], s_c.at[o], r_c, zdev(o)), source)
    own_c = lambda: pltpu.make_async_copy(trail.at[0:64, 0:256], cr.at[0], s_c.at[0])
    when(source, lambda: own_c().start())

    total = diag[z, c]
    for o in range(1, NZ):
        recv(rs_d.at[o - 1], s_rs.at[0, o - 1], r_rs.at[0, o - 1])
        total = total + rs_d[o - 1]
    d_ref[z, c] = total
    for o in ORDER_Z:
        send(lambda o=o: copy(d_ref.at[z, c], d_ref.at[z, c], s_ag.at[0, o - 1], r_ag.at[0, o - 1], zdev(o)))

    half = pl.ds(pl.multiple_of(c * 128, 128), 128)
    total = panel[z]
    for o in range(1, NZ):
        recv(rs_p.at[o - 1], s_rs.at[1, o - 1], r_rs.at[1, o - 1])
        total = total + rs_p[o - 1]
    pr[z, :, half] = total
    for o in ORDER_Z:
        send(lambda o=o: copy(pr.at[z, :, half], pr.at[z, :, half], s_ag.at[1, o - 1], r_ag.at[1, o - 1], zdev(o)))

    when(source, lambda: own_c().wait())
    recv(cr.at[z], s_c.at[0], r_c, (c == 0) & (z != 0))
    for o in ORDER_Z:
        send(lambda o=o: copy(cr.at[z], cr.at[z], s_ag.at[2, o - 1], r_ag.at[2, o - 1], zdev(o)), c == 0)

    def from_z(o):
        return lax.rem(z + NZ - o, NZ)

    for o in range(1, NZ):
        recv(d_ref.at[from_z(o), c], s_ag.at[0, o - 1], r_ag.at[0, o - 1])
    send(lambda: copy(d_ref.at[:, c], d_ref.at[:, c], s_x.at[0], r_x.at[0], other))
    recv(d_ref.at[:, 1 - c], s_x.at[0], r_x.at[0])

    for o in range(1, NZ):
        recv(pr.at[from_z(o), :, half], s_ag.at[1, o - 1], r_ag.at[1, o - 1])
    send(lambda: copy(pr.at[:, :, half], pr.at[:, :, half], s_x.at[1], r_x.at[1], other))
    recv(pr.at[:, :, half], s_x.at[1], r_x.at[1])

    for o in range(1, NZ):
        recv(cr.at[from_z(o)], s_ag.at[2, o - 1], r_ag.at[2, o - 1], c == 0)
    send(lambda: copy(cr, cr, s_x.at[2], r_x.at[2], other), c == 0)
    recv(cr, s_x.at[2], r_x.at[2], c == 1)

    @pl.when((row == 0) & (c == 0))
    def _():
        for i in range(4):
            pc0[0, 64 * i : 64 * (i + 1), :] = pr[i]

    @pl.when((row == 0) & (c == 1))
    def _():
        for i in range(4):
            pc0[1, 64 * i : 64 * (i + 1), :] = cr[i]

    def in_set(v, values):
        ok = v == values[0]
        for w in values[1:]:
            ok = ok | (v == w)
        return ok

    rows_ch = 256 // NCH
    for ch in range(NCH):
        piece = pc0.at[c, rows_ch * ch : rows_ch * (ch + 1), :]
        recv(piece, s_q.at[0, ch], r_q.at[0, ch], (x == 0) & (y != 0))
        recv(piece, s_q.at[0, ch], r_q.at[0, ch], x != 0)
        send(lambda ch=ch, piece=piece: copy(piece, piece, s_q.at[0, ch], r_q.at[0, ch], ydev(1)),
             (x == 0) & in_set(y, (0, 1, 2, 3)))
        send(lambda ch=ch, piece=piece: copy(piece, piece, s_q.at[1, ch], r_q.at[0, ch], ydev(-1)),
             (x == 0) & in_set(y, (0, 7, 6)))
        send(lambda ch=ch, piece=piece: copy(piece, piece, s_qx.at[0, ch], r_q.at[0, ch], xdev(1)),
             (x == 0) | ((x == 1) & (c == 0)))
        send(lambda ch=ch, piece=piece: copy(piece, piece, s_qx.at[1, ch], r_q.at[0, ch], xdev(-1)),
             (x == 0) | ((x == 3) & (c == 1)))
        send(lambda ch=ch, piece=piece: copy(piece, piece, s_q.at[2, ch], r_q.at[1, ch], other))

    holder = lax.rem(x, 2) == c
    middle = lax.rem(x, 2) != c
    p = lax.rem(y - 2 * lax.rem(z, 4) + NY, NY)
    tile = lax.div(z, 4)
    xh = lax.div(x, 2)
    for buf, whole in ((px, pr), (cx, cr)):
        for j in range(2):
            @pl.when(holder & (p == j))
            def _(buf=buf, whole=whole, j=j):
                for i in range(4):
                    buf[2 * j + xh, 64 * i : 64 * (i + 1), :] = whole[4 * tile + i]

    def piece_of(a, ch, k):
        return (px, cx)[a].at[k, rows_ch * ch : rows_ch * (ch + 1), :]

    plus = (in_set(p, (0, 1, 2, 3)), in_set(p, (1, 2, 3)))
    minus = (in_set(p, (0, 7, 6)), in_set(p, (1, 0, 7, 6)))
    side = (lax.div(lax.rem(x + NX - 1, NX), 2), lax.div(lax.rem(x + 1, NX), 2))
    for a in range(2):
        for ch in range(NCH):
            for j in range(2):
                own = piece_of(a, ch, 2 * j + xh)
                recv(own, s_y.at[a, ch, j, 0], r_y.at[a, ch, j], holder & (p != j))
                send(lambda own=own, a=a, ch=ch, j=j: copy(own, own, s_y.at[a, ch, j, 0], r_y.at[a, ch, j], ydev(1)),
                     holder & plus[j])
                send(lambda own=own, a=a, ch=ch, j=j: copy(own, own, s_y.at[a, ch, j, 1], r_y.at[a, ch, j], ydev(-1)),
                     holder & minus[j])
                for s in range(2):
                    send(lambda own=own, a=a, ch=ch, j=j, s=s: copy(own, own, s_t.at[a, ch, j, s], r_t.at[a, ch, j, s],
                                                                   xdev(1 - 2 * s)), holder)
            for j in range(2):
                for s in range(2):
                    got = piece_of(a, ch, 2 * j + side[s])
                    recv(got, s_t.at[a, ch, j, s], r_t.at[a, ch, j, s], middle)
                    if j == s:
                        send(lambda got=got, a=a, ch=ch, j=j, s=s: copy(got, got, s_t.at[a, ch, j, s],
                                                                       r_t.at[a, ch, j, s], xdev(1 - 2 * s)), middle)
    for a in range(2):
        for ch in range(NCH):
            for j in range(2):
                recv(piece_of(a, ch, 2 * j + 1 - xh), s_t.at[a, ch, j, j], r_t.at[a, ch, j, j], holder)
    for ch in range(NCH):
        recv(pc0.at[1 - c, rows_ch * ch : rows_ch * (ch + 1), :], s_q.at[2, ch], r_q.at[1, ch])
    for make, cond in pending:
        when(cond, lambda make=make: make().wait_send())


def compute_kernel(trail, d_ref, pr, cr, px, cx, pc0, upd, first_out, second_out, s_ref, y_ref, a1, x1, a2, x2):
    row, c, z = lax.axis_index("row"), lax.axis_index("col"), lax.axis_index("depth")
    s_ref[:, :256] = d_ref[...]
    chol_inverse(s_ref, y_ref)
    inv1 = y_ref[:, 256:]
    lead = mul_nt6(pc0[0], inv1)
    s_ref[:, :256] = pc0[1] - mul_nt6(lead, lead)
    inv1_s = split2(inv1)
    lead_s = split2(lead)
    chol_inverse(s_ref, y_ref)
    inv2_s = split2(y_ref[:, 256:])
    half = pl.ds(pl.multiple_of(c * 128, 128), 128)

    def put(ref, rows, v):
        h, m = split2(v)
        ref[0, rows, :] = h
        ref[1, rows, :] = m

    sub = lax.broadcasted_iota(jnp.int32, (256, 256), 0)
    for t in range(2):
        rows = slice(256 * t, 256 * (t + 1))
        l1 = mul_nt(split2(pr[rows, :]), inv1_s)
        put(a1, rows, l1)
        zc = cr[rows, :] - mul_nt(split2(l1), lead_s)
        l2 = mul_nt(split2(zc), inv2_s)
        y_ref[:, :256] = l1
        y_ref[:, 256:] = l2
        first_out[rows, :] = y_ref[:, half]
        second_out[rows, :] = y_ref[:, pl.ds(pl.multiple_of(256 + c * 128, 128), 128)]
        if t == 0:
            l2 = jnp.where(row == 0, jnp.zeros_like(l2), l2)
        put(a2, rows, l2)
    for k in range(4):
        rows = slice(256 * k, 256 * (k + 1))
        l1 = mul_nt(split2(px[k]), inv1_s)
        put(x1, rows, l1)
        zc = cx[k] - mul_nt(split2(l1), lead_s)
        l2 = mul_nt(split2(zc), inv2_s)
        if k == 0:
            l2 = jnp.where((c == 0) & (z == 0), jnp.zeros_like(l2), l2)
        put(x2, rows, l2)
    for k in range(4):
        rows = slice(256 * k, 256 * (k + 1))
        for t in range(2):
            mine = slice(256 * t, 256 * (t + 1))
            one = mul_nt((a1[0, mine, :], a1[1, mine, :]), (x1[0, rows, :], x1[1, rows, :]))
            two = mul_nt((a2[0, mine, :], a2[1, mine, :]), (x2[0, rows, :], x2[1, rows, :]))
            upd[mine, rows] = trail[mine, rows] - one - two


def on_device(trailing, panel_parts, diag_parts):
    vmem = pl.BlockSpec(memory_space=pltpu.VMEM)
    dma = pltpu.SemaphoreType.DMA
    shape = lambda *s: jax.ShapeDtypeStruct(s, f32)
    d_sum, pr, cr, px, cx, pc0 = pl.pallas_call(
        comm_kernel,
        out_shape=(shape(8, 2, 16, 256), shape(8, 64, 256), shape(8, 64, 256), shape(4, 256, 256), shape(4, 256, 256),
                   shape(2, 256, 256)),
        in_specs=[pl.BlockSpec(memory_space=pl.ANY), vmem, vmem],
        out_specs=[vmem] * 6,
        scratch_shapes=[
            pltpu.VMEM((7, 16, 256), f32),
            pltpu.VMEM((7, 64, 128), f32),
            dma((2, 7)), dma((2, 7)),
            dma((3, 7)), dma((3, 7)),
            dma((8,)), dma,
            dma((3,)), dma((3,)),
            dma((3, NCH)), dma((2, NCH)), dma((2, NCH)),
            dma((2, NCH, 2, 2)), dma((2, NCH, 2)),
            dma((2, NCH, 2, 2)), dma((2, NCH, 2, 2)),
        ],
        compiler_params=pltpu.CompilerParams(collective_id=0, has_side_effects=True),
        name="move",
    )(trailing, panel_parts.reshape(8, 64, 128), diag_parts.reshape(8, 2, 16, 256))
    return pl.pallas_call(
        compute_kernel,
        out_shape=(shape(512, 1024), shape(512, 128), shape(512, 128)),
        in_specs=[vmem] * 7,
        out_specs=[vmem] * 3,
        scratch_shapes=[
            pltpu.VMEM((256, 512), f32), pltpu.VMEM((256, 512), f32),
            pltpu.VMEM((2, 512, 256), bf16), pltpu.VMEM((2, 1024, 256), bf16),
            pltpu.VMEM((2, 512, 256), bf16), pltpu.VMEM((2, 1024, 256), bf16),
        ],
        name="factor",
    )(trailing, d_sum.reshape(256, 256), pr.reshape(512, 256), cr.reshape(512, 256), px, cx, pc0)


def solution(mesh):
    return jax.shard_map(
        on_device,
        mesh=mesh,
        in_specs=(P("row", ("col", "depth")), P("depth", "row", "col"), P("depth", None, None)),
        out_specs=(P("row", ("col", "depth")), P("row", "col"), P("row", "col")),
        check_vma=False,
    )
```

time: 685 us -> 144 us (0.21)
  the two profiles are of different devices: /device:TPU:64 before, /device:TPU:136 now
where the time goes in v1:
time: 144 us
  Pallas kernels  143 us (99%)
    pallas_call x1, Pallas kernels, on_device(): pl.pallas_call(comm_kernel, out_shape=(shape(8, 2, 16, 256), shape(8, 64,...  120 us
    pallas_call x1, Pallas kernels, on_device(): pl.pallas_call(compute_kernel, out_shape=(shape(512, 1024), shape(512, 12...  23.5 us

profile of v1, /device:TPU:136, one launch (start us, length us, event | category | flops | bytes accessed | tf_op | source)
XLA Modules:
  0.0 143.8 jit_solution(11618954263984841629)
XLA Ops:
  0.6 119.6 %move.1 = (f32[8,2,16,256]{3,2,1,0:T(8,128)}, f32[8,64,256]{2,1,0:T(8,128)}, f32[8,64,256]{2,1,0:T(8,128)}, f32[4,256,256]{2,1,0:T(8,128)}, f32[4,256,256]{2,1,0:T(8,128)}, /*index=5*/f32[2,256,256]{2,1,0:T(8,128)}) custom-call(f32[512,1024]{1,0:T(8,128)} %trail.3, f32[8,64,128]{2,1,0:T(8,128)} %bitcast.7, f32[8,2,16,256]{3,2,1,0:T(8,128)} %bitcast.8), custom_call_target="tpu_custom_call" | custom-call | tf_op jit(solution)/shard_map/move/pallas_call | solution.py:328
  120.3 23.5 %factor.1 = (f32[512,1024]{1,0:T(8,128)}, f32[512,128]{1,0:T(8,128)}, f32[512,128]{1,0:T(8,128)}) custom-call(f32[512,1024]{1,0:T(8,128)} %trail.3, f32[256,256]{1,0:T(8,128)} %bitcast.9, f32[512,256]{1,0:T(8,128)} %bitcast.5, f32[512,256]{1,0:T(8,128)} %bitcast.6, f32[4,256,256]{2,1,0:T(8,128)} %get-tuple-element.12.px, ...), custom_call_target="tpu_custom_call" | custom-call | tf_op jit(solution)/shard_map/factor/pallas_call | solution.py:348

commit v2 on v1

v2 whole, which is shorter than its diff:
```python
import functools
import jax
import jax.numpy as jnp
from jax import lax
from jax.experimental import pallas as pl
from jax.experimental.pallas import tpu as pltpu
from jax.sharding import PartitionSpec as P

f32, bf16 = jnp.float32, jnp.bfloat16
MESH = pl.DeviceIdType.MESH
NB = 32
NX, NY, NZ = 4, 8, 8
NCH = 2
ORDER_Z = (4, 3, 5, 2, 6, 1, 7)
N_SEM = 480


def split2(v):
    h = v.astype(bf16)
    return h, (v - h.astype(f32)).astype(bf16)


def split3(v):
    h = v.astype(bf16)
    rest = v - h.astype(f32)
    m = rest.astype(bf16)
    return h, m, (rest - m.astype(f32)).astype(bf16)


def dot_bf(a, b, dims):
    return lax.dot_general(a, b, (dims, ((), ())), preferred_element_type=f32)


NT = ((1,), (1,))


def mul_nt(a, b):
    ah, am = a
    bh, bm = b
    return dot_bf(ah, bh, NT) + (dot_bf(ah, bm, NT) + dot_bf(am, bh, NT))


def mul_nt6(a, b):
    ah, am, al = split3(a)
    bh, bm, bl = split3(b)
    low = dot_bf(am, bm, NT) + dot_bf(ah, bl, NT) + dot_bf(al, bh, NT)
    return dot_bf(ah, bh, NT) + (dot_bf(ah, bm, NT) + dot_bf(am, bh, NT) + low)


def bc_row(v, i):
    return jnp.broadcast_to(v[i : i + 1, :], (8, 128))


def factor_block(s_ref, y_ref, first):
    groups = NB // 8
    row0 = pl.multiple_of(first, NB)
    lane0 = pl.multiple_of((first // 128) * 128, 128)
    off = first % 128
    rows = [[s_ref[pl.ds(row0 + 8 * g, 8), 128 * q : 128 * (q + 1)] for q in range(4)] for g in range(groups)]
    diag = [s_ref[pl.ds(row0 + 8 * g, 8), pl.ds(lane0, 128)] for g in range(groups)]
    sub = lax.broadcasted_iota(jnp.int32, (8, 128), 0)
    cols = []
    for j in range(NB):
        idx = jnp.full((8, 128), off + j, jnp.int32)
        cols.append(
            [
                jnp.take_along_axis(diag[g], idx, axis=1, mode="promise_in_bounds") if g >= j // 8 else None
                for g in range(groups)
            ]
        )
    scale = [jnp.ones((8, 128), f32) for _ in range(groups)]
    for j in range(NB):
        gj, rj = divmod(j, 8)
        root = lax.rsqrt(bc_row(cols[j][gj], rj))
        inv = root * root
        mult = [None] * groups
        for g in range(gj, groups):
            mult[g] = cols[j][g] * inv
        for k in range(j + 1, NB):
            gk, rk = divmod(k, 8)
            b = bc_row(cols[j][gk], rk)
            for g in range(gk, groups):
                cols[k][g] = cols[k][g] - mult[g] * b
        scale[gj] = jnp.where(sub == rj, root, scale[gj])
        if rj < 7:
            mult[gj] = jnp.where(sub > rj, mult[gj], 0.0)
        for q in range(4):
            pivot = bc_row(rows[gj][q], rj)
            for g in range(gj if rj < 7 else gj + 1, groups):
                rows[g][q] = rows[g][q] - mult[g] * pivot
    for g in range(groups):
        for q in range(4):
            y_ref[pl.ds(row0 + 8 * g, 8), 128 * q : 128 * (q + 1)] = rows[g][q] * scale[g]


def chol_start(s_ref):
    i0 = lax.broadcasted_iota(jnp.int32, (256, 256), 0)
    i1 = lax.broadcasted_iota(jnp.int32, (256, 256), 1)
    s_ref[:, 256:] = jnp.where(i0 == i1, 1.0, 0.0).astype(f32)


def chol_steps(s_ref, y_ref, lo, hi):
    def body(b, carry):
        first = b * NB
        factor_block(s_ref, y_ref, first)
        h, m, l = split3(y_ref[pl.ds(pl.multiple_of(first, NB), NB), :])
        left = jnp.concatenate([h, h, m, h, m, l], axis=0)[:, :256]
        right = jnp.concatenate([h, m, h, l, m, h], axis=0)
        s_ref[...] -= dot_bf(left, right, ((0,), (0,)))
        return carry

    lax.fori_loop(lo, hi, body, 0)


def in_set(v, values):
    ok = v == values[0]
    for w in values[1:]:
        ok = ok | (v == w)
    return ok


def step_kernel(trail, panel, diag, upd, first_out, second_out, q, zq, part, rs_p, rr, px, cx, t_ref, s_ref, y_ref, a1, x1, a2, x2,
                sem, loc):
    row, c, z = lax.axis_index("row"), lax.axis_index("col"), lax.axis_index("depth")
    x, y = lax.rem(row, NX), lax.div(row, NX)
    other = (row, 1 - c, z)
    zdev = lambda o: (row, c, lax.rem(z + o + NZ, NZ))
    xdev = lambda s: (y * NX + lax.rem(x + s + NX, NX), c, z)
    ydev = lambda s: (lax.rem(y + s + NY, NY) * NX + x, c, z)
    half = pl.ds(pl.multiple_of(c * 128, 128), 128)
    origin = row == 0
    corner = origin & (c == 0) & (z == 0)

    get_trail = pltpu.make_async_copy(trail, t_ref, loc.at[0])
    get_trail.start()

    barrier = pltpu.get_barrier_semaphore()
    greet = lambda dev: pl.semaphore_signal(barrier, inc=1, device_id=dev, device_id_type=MESH)
    peers = [zdev(o) for o in range(1, NZ)] + [(row, 1 - c, lax.rem(z + o, NZ)) for o in range(NZ)]
    peers += [xdev(o) for o in range(1, NX)] + [ydev(o) for o in range(1, NY)]
    for peer in peers:
        greet(peer)

    @pl.when(row != 0)
    def _():
        greet((0, c, z))

    @pl.when((row != 0) & (c == 1) & (z == 0))
    def _():
        greet((0, 0, 0))

    extra = jnp.where(origin, NX * NY - 1, 0) + jnp.where(corner, NX * NY - 1, 0)
    pl.semaphore_wait(barrier, len(peers) + extra)

    counter = [0]
    pending = []

    def new(n=1):
        counter[0] += n
        assert counter[0] <= N_SEM
        return counter[0] - n

    def copy(src, dst, ssem, rsem, dev):
        return pltpu.make_async_remote_copy(src_ref=src, dst_ref=dst, send_sem=sem.at[ssem], recv_sem=sem.at[rsem],
                                            device_id=dev, device_id_type=MESH)

    def when(cond, fn):
        if cond is None:
            fn()
        else:
            pl.when(cond)(fn)

    def send_all(items, cond=None):
        makes = []
        for src, dst, rsem, dev in items:
            makes.append(functools.partial(copy, src, dst, new(), rsem, dev))

        def begin():
            for make in makes:
                make().start()

        when(cond, begin)
        for group in pending:
            if group[0] is cond:
                group[1].extend(makes)
                return
        pending.append((cond, makes))

    def send(src, dst, rsem, dev, cond=None):
        send_all([(src, dst, rsem, dev)], cond)

    def recv(dst, rsem, cond=None):
        when(cond, lambda: copy(dst, dst, rsem, rsem, other).wait_recv())

    r_z = new(21)
    for o in ORDER_Z:
        send(diag.at[row, :, half], zq.at[0, o - 1], r_z + o - 1, zdev(o))
    r_p0 = new()
    send_all([(panel.at[i], part, r_p0, (i, c, z)) for i in range(NX * NY - 1, 0, -1)], origin)
    r_c0 = new()
    halves = [(i, 128 * h, h) for i in range(NX * NY - 1, -1, -1) for h in range(2) if i or h]
    send_all([(trail.at[8 * i : 8 * i + 8, w : w + 128], q.at[2, i, :, w : w + 128], r_c0, (i, h, 0)) for i, w, h in halves],
             corner)
    own_c0 = lambda: pltpu.make_async_copy(trail.at[0:8, 0:128], q.at[2, 0, :, 0:128], loc.at[1])
    when(corner, lambda: own_c0().start())

    source = (c == 0) & (z == 0)
    xh, xp = lax.div(x, 2), lax.rem(x, 2)
    jy, qy = lax.rem(y, 2), lax.div(y, 2)
    mine = 2 * jy + xh
    r_ct = new()
    for t in range(2):
        home = (row, xp, qy + 4 * t)
        here = (xp == 0) & (qy + 4 * t == 0)
        tile_t = trail.at[256 * t : 256 * (t + 1), 0:256]
        send(tile_t, cx.at[mine], r_ct, home, source & jnp.logical_not(here))
        if t == 0:
            own_ct = lambda: pltpu.make_async_copy(trail.at[0:256, 0:256], cx.at[mine], loc.at[2])
            when(source & here, lambda: own_ct().start())
    r_rs = new(7)
    for o in ORDER_Z:
        to = lax.rem(z + o, NZ)
        send(panel.at[pl.ds(8 * to, 8)], rs_p.at[o - 1], r_rs + o - 1, zdev(o))
    r_cs = new()
    halves = [(i, 128 * h, h) for i in range(NZ - 1, -1, -1) for h in range(2) if i or h]
    send_all([(trail.at[64 * i : 64 * (i + 1), w : w + 128], rr.at[1, i, :, w : w + 128], r_cs, (row, h, i))
              for i, w, h in halves], source)
    own_cs = lambda: pltpu.make_async_copy(trail.at[0:64, 0:128], rr.at[1, 0, :, 0:128], loc.at[3])
    when(source, lambda: own_cs().start())

    r_qx, r_qy, r_qc = new(9), new(21), new(3)
    from_x = lambda o: y * NX + lax.rem(x + NX - o, NX)
    from_y = lambda o: lax.rem(y + NY - o, NY)

    def x_gather(a):
        piece = q.at[a, row, :, half]
        for o in (2, 1, 3):
            send(piece, piece, r_qx + 3 * a + o - 1, xdev(o))

    def y_gather(a):
        for o in range(1, NX):
            recv(q.at[a, from_x(o), :, half], r_qx + 3 * a + o - 1)
        piece = q.at[a, pl.ds(y * NX, NX), :, half]
        for o in (4, 3, 5, 2, 6, 1, 7):
            send(piece, piece, r_qy + 7 * a + o - 1, ydev(o))

    def core_gather(a):
        for o in range(1, NY):
            recv(q.at[a, pl.ds(from_y(o) * NX, NX), :, half], r_qy + 7 * a + o - 1)
        send(q.at[a, :, :, half], q.at[a, :, :, half], r_qc + a, other)

    def core_wait(a):
        recv(q.at[a, :, :, half], r_qc + a)

    def z_sum(a, own):
        total = own
        for o in range(1, NZ):
            recv(zq.at[a, o - 1], r_z + 7 * a + o - 1)
            total = total + zq[a, o - 1]
        q[a, row, :, half] = total

    z_sum(0, diag[row, :, half])
    x_gather(0)

    @pl.when(origin)
    def _():
        part[...] = panel[0]

    recv(part, r_p0, row != 0)
    for o in ORDER_Z:
        send(part, zq.at[1, o - 1], r_z + 7 + o - 1, zdev(o))
    when(corner, lambda: own_c0().wait())
    slice_c0 = q.at[2, row, :, half]
    recv(slice_c0, r_c0, (z == 0) & jnp.logical_not(corner))
    r_cz = new()
    send_all([(slice_c0, slice_c0, r_cz, zdev(o)) for o in ORDER_Z], z == 0)
    y_gather(0)
    z_sum(1, part[...])
    x_gather(1)
    recv(slice_c0, r_cz, z != 0)
    x_gather(2)

    holder = xp == c
    middle = xp != c
    p = lax.rem(y - 2 * lax.rem(z, 4) + NY, NY)
    rows_ch = 256 // NCH
    bufs = (px, cx)
    plus = (in_set(p, (0, 1, 2, 3)), in_set(p, (1, 2, 3)))
    minus = (in_set(p, (0, 7, 6)), in_set(p, (1, 0, 7, 6)))
    side = (lax.div(lax.rem(x + NX - 1, NX), 2), lax.div(lax.rem(x + 1, NX), 2))
    r_y = new(4 * NCH)
    r_x = new(8 * NCH)

    def at_y(a, ch, j):
        return r_y + (a * NCH + ch) * 2 + j

    def at_x(a, ch, j, s):
        return r_x + ((a * NCH + ch) * 2 + j) * 2 + s

    def piece_of(a, ch, k):
        return bufs[a].at[k, rows_ch * ch : rows_ch * (ch + 1), :]

    first = [holder & (p == j) for j in range(2)]
    later = [holder & (p != j) for j in range(2)]
    first_p = [first[j] & plus[j] for j in range(2)]
    first_m = [first[j] & minus[j] for j in range(2)]
    later_p = [later[j] & plus[j] for j in range(2)]
    later_m = [later[j] & minus[j] for j in range(2)]

    def spread_piece(a, ch, j, cond, cond_p, cond_m):
        own = piece_of(a, ch, 2 * j + xh)
        send(own, own, at_y(a, ch, j), ydev(1), cond_p)
        send(own, own, at_y(a, ch, j), ydev(-1), cond_m)
        send_all([(own, own, at_x(a, ch, j, s), xdev(1 - 2 * s)) for s in range(2)], cond)

    def tile_source(a):
        for ch in range(NCH):
            for j in range(2):
                spread_piece(a, ch, j, first[j], first_p[j], first_m[j])

    def tile_hop(a, ch):
        for j in range(2):
            recv(piece_of(a, ch, 2 * j + xh), at_y(a, ch, j), later[j])
            spread_piece(a, ch, j, later[j], later_p[j], later_m[j])
        for j in range(2):
            for s in range(2):
                got = piece_of(a, ch, 2 * j + side[s])
                recv(got, at_x(a, ch, j, s), middle)
                if j == s:
                    send(got, got, at_x(a, ch, j, s), xdev(1 - 2 * s), middle)

    def tile_last(a, ch):
        for j in range(2):
            recv(piece_of(a, ch, 2 * j + 1 - xh), at_x(a, ch, j, j), holder)

    root = holder & (jy == p)
    here = source & (xp == 0) & (qy == 0)
    when(here, lambda: own_ct().wait())
    recv(cx.at[mine], r_ct, root & jnp.logical_not(here))
    tile_source(1)

    total = panel[pl.ds(8 * z, 8)].reshape(64, 128)
    for o in range(1, NZ):
        recv(rs_p.at[o - 1], r_rs + o - 1)
        total = total + rs_p[o - 1].reshape(64, 128)
    rr[0, z, :, half] = total
    z4, zt = lax.rem(z, 4), lax.div(z, 4)
    at_home = px.at[mine, pl.ds(64 * z4, 64), half]
    is_home = (z == qy + 4 * zt) & (c == xp)
    r_pt = new(8)
    slot = r_pt + 2 * z4 + c
    send(rr.at[0, z, :, half], at_home, slot, (row, xp, qy + 4 * zt), jnp.logical_not(is_home))

    @pl.when(is_home)
    def _():
        px[mine, pl.ds(64 * z4, 64), half] = rr[0, z, :, half]

    when(source, lambda: own_cs().wait())
    recv(rr.at[1, z, :, half], r_cs, jnp.logical_not(source))
    r_rp, r_rm, r_rc = new(4), new(3), new()

    def ring_piece(i):
        return rr.at[:, lax.rem(z + i + NZ, NZ), :, half]

    send(ring_piece(0), ring_piece(0), r_rp, zdev(1))
    send(ring_piece(0), ring_piece(0), r_rm, zdev(-1))

    def ring(s):
        recv(ring_piece(-s), r_rp + s - 1)
        if s < 4:
            send(ring_piece(-s), ring_piece(-s), r_rp + s, zdev(1))
        if s < 4:
            recv(ring_piece(s), r_rm + s - 1)
        if s < 3:
            send(ring_piece(s), ring_piece(s), r_rm + s, zdev(-1))

    y_gather(1)
    y_gather(2)
    for i in range(4):
        for h in range(2):
            same = (z4 == i) & (c == h)
            recv(px.at[mine, 64 * i : 64 * (i + 1), 128 * h : 128 * (h + 1)], r_pt + 2 * i + h, root & jnp.logical_not(same))
    tile_source(0)
    core_gather(0)
    core_wait(0)

    s_ref[:, :256] = q[0].reshape(256, 256)
    chol_start(s_ref)
    chol_steps(s_ref, y_ref, 0, 4)
    tile_hop(1, 0)
    ring(1)
    chol_steps(s_ref, y_ref, 4, 8)
    tile_hop(1, 1)
    core_gather(1)
    core_gather(2)
    ring(2)
    core_wait(1)
    core_wait(2)
    inv1 = y_ref[:, 256:]
    lead = mul_nt6(q[1].reshape(256, 256), inv1)
    s_ref[:, :256] = q[2].reshape(256, 256) - mul_nt6(lead, lead)
    inv1_s = split2(inv1)
    lead_s = split2(lead)

    chol_start(s_ref)
    chol_steps(s_ref, y_ref, 0, 3)
    tile_hop(0, 0)
    ring(3)
    chol_steps(s_ref, y_ref, 3, 6)
    tile_hop(0, 1)
    ring(4)
    send(rr.at[:, :, :, half], rr.at[:, :, :, half], r_rc, other)
    chol_steps(s_ref, y_ref, 6, 8)
    inv2_s = split2(y_ref[:, 256:])
    recv(rr.at[:, :, :, half], r_rc)

    def put(ref, rows, v):
        h, m = split2(v)
        ref[0, rows, :] = h
        ref[1, rows, :] = m

    for t in range(2):
        rows = slice(256 * t, 256 * (t + 1))
        l1 = mul_nt(split2(rr[0, 4 * t : 4 * t + 4].reshape(256, 256)), inv1_s)
        put(a1, rows, l1)
        zc = rr[1, 4 * t : 4 * t + 4].reshape(256, 256) - mul_nt(split2(l1), lead_s)
        l2 = mul_nt(split2(zc), inv2_s)
        y_ref[:, :256] = l1
        y_ref[:, 256:] = l2
        first_out[rows, :] = y_ref[:, half]
        second_out[rows, :] = y_ref[:, pl.ds(pl.multiple_of(256 + c * 128, 128), 128)]
        if t == 0:
            l2 = jnp.where(row == 0, jnp.zeros_like(l2), l2)
        put(a2, rows, l2)
    for a in (1, 0):
        for ch in range(NCH):
            tile_last(a, ch)
    get_trail.wait()
    for k in range(4):
        rows = slice(256 * k, 256 * (k + 1))
        l1 = mul_nt(split2(px[k]), inv1_s)
        put(x1, rows, l1)
        zc = cx[k] - mul_nt(split2(l1), lead_s)
        l2 = mul_nt(split2(zc), inv2_s)
        if k == 0:
            l2 = jnp.where((c == 0) & (z == 0), jnp.zeros_like(l2), l2)
        put(x2, rows, l2)
        for t in range(2):
            mine_t = slice(256 * t, 256 * (t + 1))
            one = mul_nt((a1[0, mine_t, :], a1[1, mine_t, :]), (x1[0, rows, :], x1[1, rows, :]))
            two = mul_nt((a2[0, mine_t, :], a2[1, mine_t, :]), (x2[0, rows, :], x2[1, rows, :]))
            upd[mine_t, rows] = t_ref[mine_t, rows] - one - two

    def finish(makes):
        for make in makes:
            make().wait_send()

    for cond, makes in pending:
        when(cond, functools.partial(finish, makes))


def on_device(trailing, panel_parts, diag_parts):
    vmem = pl.BlockSpec(memory_space=pltpu.VMEM)
    dma = pltpu.SemaphoreType.DMA
    shape = lambda *s: jax.ShapeDtypeStruct(s, f32)
    return pl.pallas_call(
        step_kernel,
        out_shape=(shape(512, 1024), shape(512, 128), shape(512, 128)),
        in_specs=[pl.BlockSpec(memory_space=pl.ANY), vmem, vmem],
        out_specs=[vmem] * 3,
        scratch_shapes=[
            pltpu.VMEM((3, 32, 8, 256), f32), pltpu.VMEM((2, 7, 8, 128), f32), pltpu.VMEM((8, 128), f32),
            pltpu.VMEM((7, 8, 8, 128), f32), pltpu.VMEM((2, 8, 64, 256), f32),
            pltpu.VMEM((4, 256, 256), f32), pltpu.VMEM((4, 256, 256), f32), pltpu.VMEM((512, 1024), f32),
            pltpu.VMEM((256, 512), f32), pltpu.VMEM((256, 512), f32),
            pltpu.VMEM((2, 512, 256), bf16), pltpu.VMEM((2, 1024, 256), bf16),
            pltpu.VMEM((2, 512, 256), bf16), pltpu.VMEM((2, 1024, 256), bf16),
            dma((N_SEM,)), dma((4,)),
        ],
        compiler_params=pltpu.CompilerParams(collective_id=0, has_side_effects=True),
        name="step",
    )(trailing, panel_parts.reshape(64, 8, 128), diag_parts.reshape(32, 8, 256))


def solution(mesh):
    return jax.shard_map(
        on_device,
        mesh=mesh,
        in_specs=(P("row", ("col", "depth")), P("depth", "row", "col"), P("depth", None, None)),
        out_specs=(P("row", ("col", "depth")), P("row", "col"), P("row", "col")),
        check_vma=False,
    )
```

time: 144 us -> 98.1 us (0.68)
  Pallas kernels: 143 us -> 92.6 us
  local copies, waits for them, and re-layouts: 0 us -> 4.63 us
    pallas_call x2 -> x1, Pallas kernels: 143 us -> 92.6 us  [on_device(): pl.pallas_call(step_kernel, out_shape=(shape(512, 1024), shape(512, 128),...]
    unnamed x0 -> x7, local copies, waits for them, and re-layouts: none -> 4.63 us
where the time goes in v2:
time: 98.1 us; the launch traced here: 97.9 us
  Pallas kernels  92.6 us (94%)
  local copies, waits for them, and re-layouts  4.63 us (5%)
    pallas_call x1, Pallas kernels, on_device(): pl.pallas_call(step_kernel, out_shape=(shape(512, 1024), shape(512, 128),...  92.6 us
    unnamed x7, local copies, waits for them, and re-layouts  4.63 us

profile of v2, /device:TPU:136, one launch (start us, length us, event | category | flops | bytes accessed | tf_op | source)
XLA Modules:
  0.0 97.9 jit_solution(17945858149416882565)
XLA Ops:
  0.6 92.6 %step.1 = (f32[512,1024]{1,0:T(8,128)}, f32[512,128]{1,0:T(8,128)}, f32[512,128]{1,0:T(8,128)}) custom-call(f32[512,1024]{1,0:T(8,128)} %trail.1, f32[64,8,128]{2,1,0:T(8,128)} %bitcast.2, f32[32,8,256]{2,1,0:T(8,128)} %bitcast.3), custom_call_target="tpu_custom_call" | custom-call | tf_op jit(solution)/shard_map/step/pallas_call | solution.py:466
  93.2 0.0 copy-start.1
  93.3 0.0 copy-start
  93.3 3.2 %copy.9 = f32[512,1024]{1,0:T(8,128)} copy(f32[512,1024]{1,0:T(8,128)} %get-tuple-element.6) | data formatting | bytes 4194304
  96.5 0.0 copy-done.1
  96.5 0.7 copy.10
  97.2 0.0 copy-done
  97.2 0.7 copy.11
Async XLA Ops:
  93.2 3.2 %copy-start.1 = (f32[512,128]{1,0:T(8,128)S(1)}, f32[512,128]{1,0:T(8,128)}, u32[]{:S(2)}) copy-start(f32[512,128]{1,0:T(8,128)} %get-tuple-element.7) | copy-start | bytes 786436
  93.3 3.9 %copy-start = (f32[512,128]{1,0:T(8,128)S(1)}, f32[512,128]{1,0:T(8,128)}, u32[]{:S(2)}) copy-start(f32[512,128]{1,0:T(8,128)} %get-tuple-element.8) | copy-start | bytes 786436

commit v3 on v2

--- a/solution.py
+++ b/solution.py
@@ -34,10 +34,18 @@
 NT = ((1,), (1,))
 
 
-def mul_nt(a, b):
-    ah, am = a
-    bh, bm = b
-    return dot_bf(ah, bh, NT) + (dot_bf(ah, bm, NT) + dot_bf(am, bh, NT))
+def wide_left(v):
+    h, m = split2(v)
+    return jnp.concatenate([h, h, m], axis=1)
+
+
+def wide_right(v):
+    h, m = split2(v)
+    return jnp.concatenate([h, m, h], axis=1)
+
+
+def wide_mul(v, right):
+    return dot_bf(wide_left(v), right, NT)
 
 
 def mul_nt6(a, b):
@@ -119,8 +127,7 @@
     return ok
 
 
-def step_kernel(trail, panel, diag, upd, first_out, second_out, q, zq, part, rs_p, rr, px, cx, t_ref, s_ref, y_ref, a1, x1, a2, x2,
-                sem, loc):
+def step_kernel(trail, panel, diag, l1r, l2r, l1x, l2x, q, zq, part, rs_p, rr, px, cx, s_ref, y_ref, sem, loc):
     row, c, z = lax.axis_index("row"), lax.axis_index("col"), lax.axis_index("depth")
     x, y = lax.rem(row, NX), lax.div(row, NX)
     other = (row, 1 - c, z)
@@ -131,9 +138,6 @@
     origin = row == 0
     corner = origin & (c == 0) & (z == 0)
 
-    get_trail = pltpu.make_async_copy(trail, t_ref, loc.at[0])
-    get_trail.start()
-
     barrier = pltpu.get_barrier_semaphore()
     greet = lambda dev: pl.semaphore_signal(barrier, inc=1, device_id=dev, device_id_type=MESH)
     peers = [zdev(o) for o in range(1, NZ)] + [(row, 1 - c, lax.rem(z + o, NZ)) for o in range(NZ)]
@@ -160,7 +164,7 @@
         assert counter[0] <= N_SEM
         return counter[0] - n
 
-    def copy(src, dst, ssem, rsem, dev):
+    def copy(src, dst, rsem, dev, ssem):
         return pltpu.make_async_remote_copy(src_ref=src, dst_ref=dst, send_sem=sem.at[ssem], recv_sem=sem.at[rsem],
                                             device_id=dev, device_id_type=MESH)
 
@@ -170,16 +174,17 @@
         else:
             pl.when(cond)(fn)
 
-    def send_all(items, cond=None):
+    def send_all(items, cond=None, inside=False):
         makes = []
-        for src, dst, rsem, dev in items:
-            makes.append(functools.partial(copy, src, dst, new(), rsem, dev))
+        for item in items:
+            ssem = new()
+            makes.append(lambda item=item, ssem=ssem: copy(*(item() if inside else item), ssem))
 
         def begin():
             for make in makes:
                 make().start()
 
-        when(cond, begin)
+        when(None if inside else cond, begin)
         for group in pending:
             if group[0] is cond:
                 group[1].extend(makes)
@@ -190,7 +195,7 @@
         send_all([(src, dst, rsem, dev)], cond)
 
     def recv(dst, rsem, cond=None):
-        when(cond, lambda: copy(dst, dst, rsem, rsem, other).wait_recv())
+        when(cond, lambda: copy(dst, dst, rsem, other, rsem).wait_recv())
 
     r_z = new(21)
     for o in ORDER_Z:
@@ -259,8 +264,87 @@
             total = total + zq[a, o - 1]
         q[a, row, :, half] = total
 
+    holder = xp == c
+    middle = xp != c
+    p = lax.rem(y - 2 * lax.rem(z, 4) + NY, NY)
+    rows_ch = 256 // NCH
+    bufs = (px, cx)
+    near, mid_far, far = in_set(p, (0, 1, 2, 7)), in_set(p, (3, 6)), in_set(p, (4, 5))
+    away = jnp.where(in_set(p, (1, 2, 3)), 1, -1)
+    side = (lax.div(lax.rem(x + NX - 1, NX), 2), lax.div(lax.rem(x + 1, NX), 2))
+    r_y = new(4 * NCH)
+    r_x = new(8 * NCH)
+    root = holder & (jy == p)
+    hold_class = [holder & near, holder & mid_far, holder & far]
+    hold_near = [holder & near & (p != j) for j in range(2)]
+    mid_class = [middle & near, middle & mid_far, middle & far]
+
+    def at_y(a, ch, j):
+        return r_y + (a * NCH + ch) * 2 + j
+
+    def at_x(a, ch, j, s):
+        return r_x + ((a * NCH + ch) * 2 + j) * 2 + s
+
+    def piece_of(a, ch, k):
+        return bufs[a].at[k, rows_ch * ch : rows_ch * (ch + 1), :]
+
+    def tile_source(a):
+        items = []
+        for ch in range(NCH):
+            own = piece_of(a, ch, mine)
+            items += [(own, own, at_y(a, ch, jy), ydev(d)) for d in (1, -1)]
+            items += [(own, own, at_x(a, ch, jy, s), xdev(1 - 2 * s)) for s in range(2)]
+        send_all(items, root)
+
+    def hop(a, chs, k):
+        def one(ch, j, cond):
+            own = lambda: piece_of(a, ch, 2 * j + xh)
+            recv(own(), at_y(a, ch, j))
+            items = [lambda: (own(), own(), at_y(a, ch, j), ydev(away))] if k < 2 else []
+            items += [lambda s=s: (own(), own(), at_x(a, ch, j, s), xdev(1 - 2 * s)) for s in range(2)]
+            send_all(items, cond, True)
+
+        if k == 0:
+            for j in range(2):
+
+                @pl.when(hold_near[j])
+                def _(j=j):
+                    for ch in chs:
+                        one(ch, j, hold_near[j])
+        else:
+
+            @pl.when(hold_class[k])
+            def _():
+                for ch in chs:
+                    for j in range(2):
+                        one(ch, j, hold_class[k])
+
+    def pass_x(a, chs, k):
+        @pl.when(mid_class[k])
+        def _():
+            for ch in chs:
+                for j in range(2):
+                    for s in range(2):
+                        got = lambda ch=ch, j=j, s=s: piece_of(a, ch, 2 * j + side[s])
+                        item = lambda ch=ch, j=j, s=s, got=got: (got(), got(), at_x(a, ch, j, s), xdev(1 - 2 * s))
+                        recv(got(), at_x(a, ch, j, s))
+                        if j == s:
+                            send_all([item], mid_class[k], True)
+
+    def tile_last(a):
+        @pl.when(holder)
+        def _():
+            for ch in range(NCH):
+                for j in range(2):
+                    recv(piece_of(a, ch, 2 * j + 1 - xh), at_x(a, ch, j, j))
+
+    both = tuple(range(NCH))
     z_sum(0, diag[row, :, half])
     x_gather(0)
+    here = source & (xp == 0) & (qy == 0)
+    when(here, lambda: own_ct().wait())
+    recv(cx.at[mine], r_ct, root & jnp.logical_not(here))
+    tile_source(1)
 
     @pl.when(origin)
     def _():
@@ -275,69 +359,11 @@
     r_cz = new()
     send_all([(slice_c0, slice_c0, r_cz, zdev(o)) for o in ORDER_Z], z == 0)
     y_gather(0)
+    hop(1, both, 0)
     z_sum(1, part[...])
     x_gather(1)
     recv(slice_c0, r_cz, z != 0)
     x_gather(2)
-
-    holder = xp == c
-    middle = xp != c
-    p = lax.rem(y - 2 * lax.rem(z, 4) + NY, NY)
-    rows_ch = 256 // NCH
-    bufs = (px, cx)
-    plus = (in_set(p, (0, 1, 2, 3)), in_set(p, (1, 2, 3)))
-    minus = (in_set(p, (0, 7, 6)), in_set(p, (1, 0, 7, 6)))
-    side = (lax.div(lax.rem(x + NX - 1, NX), 2), lax.div(lax.rem(x + 1, NX), 2))
-    r_y = new(4 * NCH)
-    r_x = new(8 * NCH)
-
-    def at_y(a, ch, j):
-        return r_y + (a * NCH + ch) * 2 + j
-
-    def at_x(a, ch, j, s):
-        return r_x + ((a * NCH + ch) * 2 + j) * 2 + s
-
-    def piece_of(a, ch, k):
-        return bufs[a].at[k, rows_ch * ch : rows_ch * (ch + 1), :]
-
-    first = [holder & (p == j) for j in range(2)]
-    later = [holder & (p != j) for j in range(2)]
-    first_p = [first[j] & plus[j] for j in range(2)]
-    first_m = [first[j] & minus[j] for j in range(2)]
-    later_p = [later[j] & plus[j] for j in range(2)]
-    later_m = [later[j] & minus[j] for j in range(2)]
-
-    def spread_piece(a, ch, j, cond, cond_p, cond_m):
-        own = piece_of(a, ch, 2 * j + xh)
-        send(own, own, at_y(a, ch, j), ydev(1), cond_p)
-        send(own, own, at_y(a, ch, j), ydev(-1), cond_m)
-        send_all([(own, own, at_x(a, ch, j, s), xdev(1 - 2 * s)) for s in range(2)], cond)
-
-    def tile_source(a):
-        for ch in range(NCH):
-            for j in range(2):
-                spread_piece(a, ch, j, first[j], first_p[j], first_m[j])
-
-    def tile_hop(a, ch):
-        for j in range(2):
-            recv(piece_of(a, ch, 2 * j + xh), at_y(a, ch, j), later[j])
-            spread_piece(a, ch, j, later[j], later_p[j], later_m[j])
-        for j in range(2):
-            for s in range(2):
-                got = piece_of(a, ch, 2 * j + side[s])
-                recv(got, at_x(a, ch, j, s), middle)
-                if j == s:
-                    send(got, got, at_x(a, ch, j, s), xdev(1 - 2 * s), middle)
-
-    def tile_last(a, ch):
-        for j in range(2):
-            recv(piece_of(a, ch, 2 * j + 1 - xh), at_x(a, ch, j, j), holder)
-
-    root = holder & (jy == p)
-    here = source & (xp == 0) & (qy == 0)
-    when(here, lambda: own_ct().wait())
-    recv(cx.at[mine], r_ct, root & jnp.logical_not(here))
-    tile_source(1)
 
     total = panel[pl.ds(8 * z, 8)].reshape(64, 128)
     for o in range(1, NZ):
@@ -369,87 +395,76 @@
         recv(ring_piece(-s), r_rp + s - 1)
         if s < 4:
             send(ring_piece(-s), ring_piece(-s), r_rp + s, zdev(1))
-        if s < 4:
             recv(ring_piece(s), r_rm + s - 1)
         if s < 3:
             send(ring_piece(s), ring_piece(s), r_rm + s, zdev(-1))
 
+    hop(1, both, 1)
+    core_gather(0)
     y_gather(1)
     y_gather(2)
-    for i in range(4):
-        for h in range(2):
-            same = (z4 == i) & (c == h)
-            recv(px.at[mine, 64 * i : 64 * (i + 1), 128 * h : 128 * (h + 1)], r_pt + 2 * i + h, root & jnp.logical_not(same))
+
+    @pl.when(root)
+    def _():
+        for i in range(4):
+            for h in range(2):
+                same = (z4 == i) & (c == h)
+                recv(px.at[mine, 64 * i : 64 * (i + 1), 128 * h : 128 * (h + 1)], r_pt + 2 * i + h, jnp.logical_not(same))
+
     tile_source(0)
-    core_gather(0)
     core_wait(0)
 
     s_ref[:, :256] = q[0].reshape(256, 256)
     chol_start(s_ref)
-    chol_steps(s_ref, y_ref, 0, 4)
-    tile_hop(1, 0)
+    pass_x(1, both, 0)
+    chol_steps(s_ref, y_ref, 0, 3)
+    hop(0, (0,), 0)
+    hop(1, both, 2)
     ring(1)
-    chol_steps(s_ref, y_ref, 4, 8)
-    tile_hop(1, 1)
+    chol_steps(s_ref, y_ref, 3, 6)
+    hop(0, both[1:], 0)
+    hop(0, (0,), 1)
+    pass_x(1, both, 1)
     core_gather(1)
     core_gather(2)
     ring(2)
+    chol_steps(s_ref, y_ref, 6, 8)
+    hop(0, both[1:], 1)
+    pass_x(0, (0,), 0)
     core_wait(1)
     core_wait(2)
     inv1 = y_ref[:, 256:]
     lead = mul_nt6(q[1].reshape(256, 256), inv1)
     s_ref[:, :256] = q[2].reshape(256, 256) - mul_nt6(lead, lead)
-    inv1_s = split2(inv1)
-    lead_s = split2(lead)
+    inv1_r = wide_right(inv1)
+    lead_r = wide_right(lead)
+    pass_x(1, both, 2)
+    ring(3)
 
     chol_start(s_ref)
-    chol_steps(s_ref, y_ref, 0, 3)
-    tile_hop(0, 0)
-    ring(3)
-    chol_steps(s_ref, y_ref, 3, 6)
-    tile_hop(0, 1)
+    chol_steps(s_ref, y_ref, 0, 2)
+    hop(0, (0,), 2)
+    pass_x(0, both[1:], 0)
+    pass_x(0, (0,), 1)
     ring(4)
     send(rr.at[:, :, :, half], rr.at[:, :, :, half], r_rc, other)
+    chol_steps(s_ref, y_ref, 2, 4)
+    hop(0, both[1:], 2)
+    pass_x(0, both[1:], 1)
+    tile_last(1)
+    chol_steps(s_ref, y_ref, 4, 6)
+    pass_x(0, both, 2)
+    recv(rr.at[:, :, :, half], r_rc)
     chol_steps(s_ref, y_ref, 6, 8)
-    inv2_s = split2(y_ref[:, 256:])
-    recv(rr.at[:, :, :, half], r_rc)
-
-    def put(ref, rows, v):
-        h, m = split2(v)
-        ref[0, rows, :] = h
-        ref[1, rows, :] = m
-
-    for t in range(2):
-        rows = slice(256 * t, 256 * (t + 1))
-        l1 = mul_nt(split2(rr[0, 4 * t : 4 * t + 4].reshape(256, 256)), inv1_s)
-        put(a1, rows, l1)
-        zc = rr[1, 4 * t : 4 * t + 4].reshape(256, 256) - mul_nt(split2(l1), lead_s)
-        l2 = mul_nt(split2(zc), inv2_s)
-        y_ref[:, :256] = l1
-        y_ref[:, 256:] = l2
-        first_out[rows, :] = y_ref[:, half]
-        second_out[rows, :] = y_ref[:, pl.ds(pl.multiple_of(256 + c * 128, 128), 128)]
-        if t == 0:
-            l2 = jnp.where(row == 0, jnp.zeros_like(l2), l2)
-        put(a2, rows, l2)
-    for a in (1, 0):
-        for ch in range(NCH):
-            tile_last(a, ch)
-    get_trail.wait()
-    for k in range(4):
-        rows = slice(256 * k, 256 * (k + 1))
-        l1 = mul_nt(split2(px[k]), inv1_s)
-        put(x1, rows, l1)
-        zc = cx[k] - mul_nt(split2(l1), lead_s)
-        l2 = mul_nt(split2(zc), inv2_s)
-        if k == 0:
-            l2 = jnp.where((c == 0) & (z == 0), jnp.zeros_like(l2), l2)
-        put(x2, rows, l2)
-        for t in range(2):
-            mine_t = slice(256 * t, 256 * (t + 1))
-            one = mul_nt((a1[0, mine_t, :], a1[1, mine_t, :]), (x1[0, rows, :], x1[1, rows, :]))
-            two = mul_nt((a2[0, mine_t, :], a2[1, mine_t, :]), (x2[0, rows, :], x2[1, rows, :]))
-            upd[mine_t, rows] = t_ref[mine_t, rows] - one - two
+    inv2_r = wide_right(y_ref[:, 256:])
+
+    l1 = wide_mul(rr[0].reshape(512, 256), inv1_r)
+    l1r[...] = l1
+    l2r[...] = wide_mul(rr[1].reshape(512, 256) - wide_mul(l1, lead_r), inv2_r)
+    tile_last(0)
+    l1 = wide_mul(px[...].reshape(1024, 256), inv1_r)
+    l1x[...] = l1
+    l2x[...] = wide_mul(cx[...].reshape(1024, 256) - wide_mul(l1, lead_r), inv2_r)
 
     def finish(makes):
         for make in makes:
@@ -457,29 +472,58 @@
 
     for cond, makes in pending:
         when(cond, functools.partial(finish, makes))
+
+
+def update_kernel(trail, l1r, l2r, l1x, l2x, upd, first_out, second_out, left):
+    row, c, z = lax.axis_index("row"), lax.axis_index("col"), lax.axis_index("depth")
+    k = pl.program_id(0)
+
+    @pl.when(k == 0)
+    def _():
+        half = pl.ds(pl.multiple_of(c * 128, 128), 128)
+        first_out[...] = l1r[:, half]
+        second_out[...] = l2r[:, half]
+        left[:, :768] = wide_left(l1r[...])
+        slot = lax.broadcasted_iota(jnp.int32, (512, 256), 0)
+        left[:, 768:] = wide_left(jnp.where((slot < 256) & (row == 0), 0.0, l2r[...]))
+
+    x2 = jnp.where((k == 0) & (c == 0) & (z == 0), 0.0, l2x[...])
+    right = jnp.concatenate([wide_right(l1x[...]), wide_right(x2)], axis=1)
+    upd[...] = trail[...] - dot_bf(left[...], right, NT)
 
 
 def on_device(trailing, panel_parts, diag_parts):
     vmem = pl.BlockSpec(memory_space=pltpu.VMEM)
     dma = pltpu.SemaphoreType.DMA
     shape = lambda *s: jax.ShapeDtypeStruct(s, f32)
-    return pl.pallas_call(
+    factors = pl.pallas_call(
         step_kernel,
-        out_shape=(shape(512, 1024), shape(512, 128), shape(512, 128)),
+        out_shape=(shape(512, 256), shape(512, 256), shape(1024, 256), shape(1024, 256)),
         in_specs=[pl.BlockSpec(memory_space=pl.ANY), vmem, vmem],
-        out_specs=[vmem] * 3,
+        out_specs=[vmem] * 4,
         scratch_shapes=[
             pltpu.VMEM((3, 32, 8, 256), f32), pltpu.VMEM((2, 7, 8, 128), f32), pltpu.VMEM((8, 128), f32),
             pltpu.VMEM((7, 8, 8, 128), f32), pltpu.VMEM((2, 8, 64, 256), f32),
-            pltpu.VMEM((4, 256, 256), f32), pltpu.VMEM((4, 256, 256), f32), pltpu.VMEM((512, 1024), f32),
+            pltpu.VMEM((4, 256, 256), f32), pltpu.VMEM((4, 256, 256), f32),
             pltpu.VMEM((256, 512), f32), pltpu.VMEM((256, 512), f32),
-            pltpu.VMEM((2, 512, 256), bf16), pltpu.VMEM((2, 1024, 256), bf16),
-            pltpu.VMEM((2, 512, 256), bf16), pltpu.VMEM((2, 1024, 256), bf16),
             dma((N_SEM,)), dma((4,)),
         ],
         compiler_params=pltpu.CompilerParams(collective_id=0, has_side_effects=True),
         name="step",
     )(trailing, panel_parts.reshape(64, 8, 128), diag_parts.reshape(32, 8, 256))
+    whole = pl.BlockSpec((512, 256), lambda k: (0, 0))
+    slab = pl.BlockSpec((512, 256), lambda k: (0, k))
+    tile = pl.BlockSpec((256, 256), lambda k: (k, 0))
+    share = pl.BlockSpec((512, 128), lambda k: (0, 0))
+    return pl.pallas_call(
+        update_kernel,
+        grid=(4,),
+        out_shape=(shape(512, 1024), shape(512, 128), shape(512, 128)),
+        in_specs=[slab, whole, whole, tile, tile],
+        out_specs=[slab, share, share],
+        scratch_shapes=[pltpu.VMEM((512, 1536), bf16)],
+        name="update",
+    )(trailing, *factors)
 
 
 def solution(mesh):

time: 98.1 us -> 87 us (0.89)
  the two profiles are of different devices: /device:TPU:136 before, /device:TPU:32 now
where the time goes in v3:
time: 87 us; the launch traced here: 86.8 us
  Pallas kernels  86.2 us (99%)
    pallas_call x1, Pallas kernels, on_device(): pl.pallas_call(step_kernel, out_shape=(shape(512, 256), shape(512, 256),...  80.2 us
    pallas_call x1, Pallas kernels, on_device(): pl.pallas_call(update_kernel, grid=(4,), out_shape=(shape(512, 1024), sha...  5.98 us

profile of v3, /device:TPU:32, one launch (start us, length us, event | category | flops | bytes accessed | tf_op | source)
XLA Modules:
  0.0 86.8 jit_solution(760436839078097449)
XLA Ops:
  0.6 80.2 %step.1 = (f32[512,256]{1,0:T(8,128)}, f32[512,256]{1,0:T(8,128)}, f32[1024,256]{1,0:T(8,128)}, f32[1024,256]{1,0:T(8,128)}) custom-call(f32[512,1024]{1,0:T(8,128)} %trail.3, f32[64,8,128]{2,1,0:T(8,128)} %bitcast.2, f32[32,8,256]{2,1,0:T(8,128)} %bitcast.3), custom_call_target="tpu_custom_call" | custom-call | tf_op jit(solution)/shard_map/step/pallas_call | solution.py:499
  80.9 6.0 %update.1 = (f32[512,1024]{1,0:T(8,128)}, f32[512,128]{1,0:T(8,128)}, f32[512,128]{1,0:T(8,128)}) custom-call(f32[512,1024]{1,0:T(8,128)} %trail.3, f32[512,256]{1,0:T(8,128)} %get-tuple-element.7.l1r, f32[512,256]{1,0:T(8,128)} %get-tuple-element.8.l2r, f32[1024,256]{1,0:T(8,128)} %get-tuple-element.9.l1x, f32[1024,256]{1,0:T(8,128)} %get-tuple-element.10.l2x), custom_call_target="tpu_custom_call" | custom-call | tf_op jit(solution)/shard_map/update/pallas_call | solution.py:518

commit v4 on v3

--- a/solution.py
+++ b/solution.py
@@ -213,6 +213,128 @@
     xh, xp = lax.div(x, 2), lax.rem(x, 2)
     jy, qy = lax.rem(y, 2), lax.div(y, 2)
     mine = 2 * jy + xh
+    r_qx, r_qy, r_qc = new(9), new(21), new(3)
+    from_x = lambda o: y * NX + lax.rem(x + NX - o, NX)
+    from_y = lambda o: lax.rem(y + NY - o, NY)
+
+    def x_gather(a):
+        piece = q.at[a, row, :, half]
+        for o in (2, 1, 3):
+            send(piece, piece, r_qx + 3 * a + o - 1, xdev(o))
+
+    def y_gather(a):
+        for o in range(1, NX):
+            recv(q.at[a, from_x(o), :, half], r_qx + 3 * a + o - 1)
+        piece = q.at[a, pl.ds(y * NX, NX), :, half]
+        for o in (4, 3, 5, 2, 6, 1, 7):
+            send(piece, piece, r_qy + 7 * a + o - 1, ydev(o))
+
+    def core_gather(a):
+        for o in range(1, NY):
+            recv(q.at[a, pl.ds(from_y(o) * NX, NX), :, half], r_qy + 7 * a + o - 1)
+        send(q.at[a, :, :, half], q.at[a, :, :, half], r_qc + a, other)
+
+    def core_wait(a):
+        recv(q.at[a, :, :, half], r_qc + a)
+
+    def z_sum(a, own):
+        total = own
+        for o in range(1, NZ):
+            recv(zq.at[a, o - 1], r_z + 7 * a + o - 1)
+            total = total + zq[a, o - 1]
+        q[a, row, :, half] = total
+
+    holder = xp == c
+    middle = xp != c
+    p = lax.rem(y - 2 * lax.rem(z, 4) + NY, NY)
+    rows_ch = 256 // NCH
+    bufs = (px, cx)
+    near, mid_far, far = in_set(p, (0, 1, 2, 7)), in_set(p, (3, 6)), in_set(p, (4, 5))
+    away = jnp.where(in_set(p, (1, 2, 3)), 1, -1)
+    side = (lax.div(lax.rem(x + NX - 1, NX), 2), lax.div(lax.rem(x + 1, NX), 2))
+    r_y = new(4 * NCH)
+    r_x = new(8 * NCH)
+    root = holder & (jy == p)
+    hold_class = [holder & near, holder & mid_far, holder & far]
+    hold_near = [holder & near & (p != j) for j in range(2)]
+    mid_class = [middle & near, middle & mid_far, middle & far]
+
+    def at_y(a, ch, j):
+        return r_y + (a * NCH + ch) * 2 + j
+
+    def at_x(a, ch, j, s):
+        return r_x + ((a * NCH + ch) * 2 + j) * 2 + s
+
+    def piece_of(a, ch, k):
+        return bufs[a].at[k, rows_ch * ch : rows_ch * (ch + 1), :]
+
+    def tile_source(a):
+        items = []
+        for ch in range(NCH):
+            own = piece_of(a, ch, mine)
+            items += [(own, own, at_y(a, ch, jy), ydev(d)) for d in (1, -1)]
+            items += [(own, own, at_x(a, ch, jy, s), xdev(1 - 2 * s)) for s in range(2)]
+        send_all(items, root)
+
+    def hop(a, chs, k):
+        def one(ch, j, cond):
+            own = lambda: piece_of(a, ch, 2 * j + xh)
+            recv(own(), at_y(a, ch, j))
+            items = [lambda: (own(), own(), at_y(a, ch, j), ydev(away))] if k < 2 else []
+            items += [lambda s=s: (own(), own(), at_x(a, ch, j, s), xdev(1 - 2 * s)) for s in range(2)]
+            send_all(items, cond, True)
+
+        if k == 0:
+            for j in range(2):
+
+                @pl.when(hold_near[j])
+                def _(j=j):
+                    for ch in chs:
+                        one(ch, j, hold_near[j])
+        else:
+
+            @pl.when(hold_class[k])
+            def _():
+                for ch in chs:
+                    for j in range(2):
+                        one(ch, j, hold_class[k])
+
+    def pass_x(a, chs, k):
+        @pl.when(mid_class[k])
+        def _():
+            for ch in chs:
+                for j in range(2):
+                    for s in range(2):
+                        got = lambda ch=ch, j=j, s=s: piece_of(a, ch, 2 * j + side[s])
+                        item = lambda ch=ch, j=j, s=s, got=got: (got(), got(), at_x(a, ch, j, s), xdev(1 - 2 * s))
+                        recv(got(), at_x(a, ch, j, s))
+                        if j == s:
+                            send_all([item], mid_class[k], True)
+
+    def tile_last(a):
+        @pl.when(holder)
+        def _():
+            for ch in range(NCH):
+                for j in range(2):
+                    recv(piece_of(a, ch, 2 * j + 1 - xh), at_x(a, ch, j, j))
+
+    both = tuple(range(NCH))
+    z_sum(0, diag[row, :, half])
+    x_gather(0)
+
+    @pl.when(origin)
+    def _():
+        part[...] = panel[0]
+
+    recv(part, r_p0, row != 0)
+    for o in ORDER_Z:
+        send(part, zq.at[1, o - 1], r_z + 7 + o - 1, zdev(o))
+    when(corner, lambda: own_c0().wait())
+    slice_c0 = q.at[2, row, :, half]
+    recv(slice_c0, r_c0, (z == 0) & jnp.logical_not(corner))
+    r_cz = new()
+    send_all([(slice_c0, slice_c0, r_cz, zdev(o)) for o in ORDER_Z], z == 0)
+
     r_ct = new()
     for t in range(2):
         home = (row, xp, qy + 4 * t)
@@ -233,163 +355,20 @@
     own_cs = lambda: pltpu.make_async_copy(trail.at[0:64, 0:128], rr.at[1, 0, :, 0:128], loc.at[3])
     when(source, lambda: own_cs().start())
 
-    r_qx, r_qy, r_qc = new(9), new(21), new(3)
-    from_x = lambda o: y * NX + lax.rem(x + NX - o, NX)
-    from_y = lambda o: lax.rem(y + NY - o, NY)
-
-    def x_gather(a):
-        piece = q.at[a, row, :, half]
-        for o in (2, 1, 3):
-            send(piece, piece, r_qx + 3 * a + o - 1, xdev(o))
-
-    def y_gather(a):
-        for o in range(1, NX):
-            recv(q.at[a, from_x(o), :, half], r_qx + 3 * a + o - 1)
-        piece = q.at[a, pl.ds(y * NX, NX), :, half]
-        for o in (4, 3, 5, 2, 6, 1, 7):
-            send(piece, piece, r_qy + 7 * a + o - 1, ydev(o))
-
-    def core_gather(a):
-        for o in range(1, NY):
-            recv(q.at[a, pl.ds(from_y(o) * NX, NX), :, half], r_qy + 7 * a + o - 1)
-        send(q.at[a, :, :, half], q.at[a, :, :, half], r_qc + a, other)
-
-    def core_wait(a):
-        recv(q.at[a, :, :, half], r_qc + a)
-
-    def z_sum(a, own):
-        total = own
-        for o in range(1, NZ):
-            recv(zq.at[a, o - 1], r_z + 7 * a + o - 1)
-            total = total + zq[a, o - 1]
-        q[a, row, :, half] = total
-
-    holder = xp == c
-    middle = xp != c
-    p = lax.rem(y - 2 * lax.rem(z, 4) + NY, NY)
-    rows_ch = 256 // NCH
-    bufs = (px, cx)
-    near, mid_far, far = in_set(p, (0, 1, 2, 7)), in_set(p, (3, 6)), in_set(p, (4, 5))
-    away = jnp.where(in_set(p, (1, 2, 3)), 1, -1)
-    side = (lax.div(lax.rem(x + NX - 1, NX), 2), lax.div(lax.rem(x + 1, NX), 2))
-    r_y = new(4 * NCH)
-    r_x = new(8 * NCH)
-    root = holder & (jy == p)
-    hold_class = [holder & near, holder & mid_far, holder & far]
-    hold_near = [holder & near & (p != j) for j in range(2)]
-    mid_class = [middle & near, middle & mid_far, middle & far]
-
-    def at_y(a, ch, j):
-        return r_y + (a * NCH + ch) * 2 + j
-
-    def at_x(a, ch, j, s):
-        return r_x + ((a * NCH + ch) * 2 + j) * 2 + s
-
-    def piece_of(a, ch, k):
-        return bufs[a].at[k, rows_ch * ch : rows_ch * (ch + 1), :]
-
-    def tile_source(a):
-        items = []
-        for ch in range(NCH):
-            own = piece_of(a, ch, mine)
-            items += [(own, own, at_y(a, ch, jy), ydev(d)) for d in (1, -1)]
-            items += [(own, own, at_x(a, ch, jy, s), xdev(1 - 2 * s)) for s in range(2)]
-        send_all(items, root)
-
-    def hop(a, chs, k):
-        def one(ch, j, cond):
-            own = lambda: piece_of(a, ch, 2 * j + xh)
-            recv(own(), at_y(a, ch, j))
-            items = [lambda: (own(), own(), at_y(a, ch, j), ydev(away))] if k < 2 else []
-            items += [lambda s=s: (own(), own(), at_x(a, ch, j, s), xdev(1 - 2 * s)) for s in range(2)]
-            send_all(items, cond, True)
-
-        if k == 0:
-            for j in range(2):
-
-                @pl.when(hold_near[j])
-                def _(j=j):
-                    for ch in chs:
-                        one(ch, j, hold_near[j])
-        else:
-
-            @pl.when(hold_class[k])
-            def _():
-                for ch in chs:
-                    for j in range(2):
-                        one(ch, j, hold_class[k])
-
-    def pass_x(a, chs, k):
-        @pl.when(mid_class[k])
-        def _():
-            for ch in chs:
-                for j in range(2):
-                    for s in range(2):
-                        got = lambda ch=ch, j=j, s=s: piece_of(a, ch, 2 * j + side[s])
-                        item = lambda ch=ch, j=j, s=s, got=got: (got(), got(), at_x(a, ch, j, s), xdev(1 - 2 * s))
-                        recv(got(), at_x(a, ch, j, s))
-                        if j == s:
-                            send_all([item], mid_class[k], True)
-
-    def tile_last(a):
-        @pl.when(holder)
-        def _():
-            for ch in range(NCH):
-                for j in range(2):
-                    recv(piece_of(a, ch, 2 * j + 1 - xh), at_x(a, ch, j, j))
-
-    both = tuple(range(NCH))
-    z_sum(0, diag[row, :, half])
-    x_gather(0)
-    here = source & (xp == 0) & (qy == 0)
-    when(here, lambda: own_ct().wait())
-    recv(cx.at[mine], r_ct, root & jnp.logical_not(here))
-    tile_source(1)
-
-    @pl.when(origin)
-    def _():
-        part[...] = panel[0]
-
-    recv(part, r_p0, row != 0)
-    for o in ORDER_Z:
-        send(part, zq.at[1, o - 1], r_z + 7 + o - 1, zdev(o))
-    when(corner, lambda: own_c0().wait())
-    slice_c0 = q.at[2, row, :, half]
-    recv(slice_c0, r_c0, (z == 0) & jnp.logical_not(corner))
-    r_cz = new()
-    send_all([(slice_c0, slice_c0, r_cz, zdev(o)) for o in ORDER_Z], z == 0)
     y_gather(0)
-    hop(1, both, 0)
     z_sum(1, part[...])
     x_gather(1)
     recv(slice_c0, r_cz, z != 0)
     x_gather(2)
-
-    total = panel[pl.ds(8 * z, 8)].reshape(64, 128)
-    for o in range(1, NZ):
-        recv(rs_p.at[o - 1], r_rs + o - 1)
-        total = total + rs_p[o - 1].reshape(64, 128)
-    rr[0, z, :, half] = total
+    y_gather(1)
+    y_gather(2)
+    core_gather(0)
     z4, zt = lax.rem(z, 4), lax.div(z, 4)
-    at_home = px.at[mine, pl.ds(64 * z4, 64), half]
-    is_home = (z == qy + 4 * zt) & (c == xp)
     r_pt = new(8)
-    slot = r_pt + 2 * z4 + c
-    send(rr.at[0, z, :, half], at_home, slot, (row, xp, qy + 4 * zt), jnp.logical_not(is_home))
-
-    @pl.when(is_home)
-    def _():
-        px[mine, pl.ds(64 * z4, 64), half] = rr[0, z, :, half]
-
-    when(source, lambda: own_cs().wait())
-    recv(rr.at[1, z, :, half], r_cs, jnp.logical_not(source))
     r_rp, r_rm, r_rc = new(4), new(3), new()
 
     def ring_piece(i):
         return rr.at[:, lax.rem(z + i + NZ, NZ), :, half]
-
-    send(ring_piece(0), ring_piece(0), r_rp, zdev(1))
-    send(ring_piece(0), ring_piece(0), r_rm, zdev(-1))
 
     def ring(s):
         recv(ring_piece(-s), r_rp + s - 1)
@@ -399,10 +378,38 @@
         if s < 3:
             send(ring_piece(s), ring_piece(s), r_rm + s, zdev(-1))
 
-    hop(1, both, 1)
-    core_gather(0)
-    y_gather(1)
-    y_gather(2)
+    core_wait(0)
+
+    s_ref[:, :256] = q[0].reshape(256, 256)
+    chol_start(s_ref)
+    chol_steps(s_ref, y_ref, 0, 2)
+    here = source & (xp == 0) & (qy == 0)
+    when(here, lambda: own_ct().wait())
+    recv(cx.at[mine], r_ct, root & jnp.logical_not(here))
+    tile_source(1)
+
+    total = panel[pl.ds(8 * z, 8)].reshape(64, 128)
+    for o in range(1, NZ):
+        recv(rs_p.at[o - 1], r_rs + o - 1)
+        total = total + rs_p[o - 1].reshape(64, 128)
+    rr[0, z, :, half] = total
+    at_home = px.at[mine, pl.ds(64 * z4, 64), half]
+    is_home = (z == qy + 4 * zt) & (c == xp)
+    slot = r_pt + 2 * z4 + c
+    send(rr.at[0, z, :, half], at_home, slot, (row, xp, qy + 4 * zt), jnp.logical_not(is_home))
+
+    @pl.when(is_home)
+    def _():
+        px[mine, pl.ds(64 * z4, 64), half] = rr[0, z, :, half]
+
+    when(source, lambda: own_cs().wait())
+    recv(rr.at[1, z, :, half], r_cs, jnp.logical_not(source))
+    send(ring_piece(0), ring_piece(0), r_rp, zdev(1))
+    send(ring_piece(0), ring_piece(0), r_rm, zdev(-1))
+    chol_steps(s_ref, y_ref, 2, 4)
+    hop(1, both, 0)
+    core_gather(1)
+    core_gather(2)
 
     @pl.when(root)
     def _():
@@ -412,25 +419,13 @@
                 recv(px.at[mine, 64 * i : 64 * (i + 1), 128 * h : 128 * (h + 1)], r_pt + 2 * i + h, jnp.logical_not(same))
 
     tile_source(0)
-    core_wait(0)
-
-    s_ref[:, :256] = q[0].reshape(256, 256)
-    chol_start(s_ref)
+    chol_steps(s_ref, y_ref, 4, 6)
+    hop(1, both, 1)
+    hop(0, (0,), 0)
+    ring(1)
+    chol_steps(s_ref, y_ref, 6, 8)
+    hop(0, both[1:], 0)
     pass_x(1, both, 0)
-    chol_steps(s_ref, y_ref, 0, 3)
-    hop(0, (0,), 0)
-    hop(1, both, 2)
-    ring(1)
-    chol_steps(s_ref, y_ref, 3, 6)
-    hop(0, both[1:], 0)
-    hop(0, (0,), 1)
-    pass_x(1, both, 1)
-    core_gather(1)
-    core_gather(2)
-    ring(2)
-    chol_steps(s_ref, y_ref, 6, 8)
-    hop(0, both[1:], 1)
-    pass_x(0, (0,), 0)
     core_wait(1)
     core_wait(2)
     inv1 = y_ref[:, 256:]
@@ -438,24 +433,30 @@
     s_ref[:, :256] = q[2].reshape(256, 256) - mul_nt6(lead, lead)
     inv1_r = wide_right(inv1)
     lead_r = wide_right(lead)
-    pass_x(1, both, 2)
-    ring(3)
+    hop(0, (0,), 1)
+    ring(2)
 
     chol_start(s_ref)
     chol_steps(s_ref, y_ref, 0, 2)
+    hop(0, both[1:], 1)
+    hop(1, both, 2)
+    pass_x(1, both, 1)
+    pass_x(0, (0,), 0)
+    ring(3)
+    chol_steps(s_ref, y_ref, 2, 4)
     hop(0, (0,), 2)
     pass_x(0, both[1:], 0)
     pass_x(0, (0,), 1)
     ring(4)
     send(rr.at[:, :, :, half], rr.at[:, :, :, half], r_rc, other)
-    chol_steps(s_ref, y_ref, 2, 4)
+    chol_steps(s_ref, y_ref, 4, 6)
     hop(0, both[1:], 2)
+    pass_x(1, both, 2)
     pass_x(0, both[1:], 1)
+    chol_steps(s_ref, y_ref, 6, 8)
     tile_last(1)
-    chol_steps(s_ref, y_ref, 4, 6)
+    recv(rr.at[:, :, :, half], r_rc)
     pass_x(0, both, 2)
-    recv(rr.at[:, :, :, half], r_rc)
-    chol_steps(s_ref, y_ref, 6, 8)
     inv2_r = wide_right(y_ref[:, 256:])
 
     l1 = wide_mul(rr[0].reshape(512, 256), inv1_r)
@@ -487,7 +488,8 @@
         slot = lax.broadcasted_iota(jnp.int32, (512, 256), 0)
         left[:, 768:] = wide_left(jnp.where((slot < 256) & (row == 0), 0.0, l2r[...]))
 
-    x2 = jnp.where((k == 0) & (c == 0) & (z == 0), 0.0, l2x[...])
+    spot = lax.broadcasted_iota(jnp.int32, (512, 256), 0)
+    x2 = jnp.where((spot < 256) & (k == 0) & (c == 0) & (z == 0), 0.0, l2x[...])
     right = jnp.concatenate([wide_right(l1x[...]), wide_right(x2)], axis=1)
     upd[...] = trail[...] - dot_bf(left[...], right, NT)
 
@@ -512,12 +514,12 @@
         name="step",
     )(trailing, panel_parts.reshape(64, 8, 128), diag_parts.reshape(32, 8, 256))
     whole = pl.BlockSpec((512, 256), lambda k: (0, 0))
-    slab = pl.BlockSpec((512, 256), lambda k: (0, k))
-    tile = pl.BlockSpec((256, 256), lambda k: (k, 0))
+    slab = pl.BlockSpec((512, 512), lambda k: (0, k))
+    tile = pl.BlockSpec((512, 256), lambda k: (k, 0))
     share = pl.BlockSpec((512, 128), lambda k: (0, 0))
     return pl.pallas_call(
         update_kernel,
-        grid=(4,),
+        grid=(2,),
         out_shape=(shape(512, 1024), shape(512, 128), shape(512, 128)),
         in_specs=[slab, whole, whole, tile, tile],
         out_specs=[slab, share, share],

time: 87 us -> 90.4 us (1.039)
  the two profiles are of different devices: /device:TPU:32 before, /device:TPU:136 now
where the time goes in v4:
time: 90.4 us; the launch traced here: 90.2 us
  Pallas kernels  89.6 us (99%)
    pallas_call x1, Pallas kernels, on_device(): pl.pallas_call(step_kernel, out_shape=(shape(512, 256), shape(512, 256),...  84.4 us
    pallas_call x1, Pallas kernels, on_device(): pl.pallas_call(update_kernel, grid=(2,), out_shape=(shape(512, 1024), sha...  5.23 us

profile of v4, /device:TPU:136, one launch (start us, length us, event | category | flops | bytes accessed | tf_op | source)
XLA Modules:
  0.0 90.2 jit_solution(652701730738694248)
XLA Ops:
  0.6 84.4 %step.1 = (f32[512,256]{1,0:T(8,128)}, f32[512,256]{1,0:T(8,128)}, f32[1024,256]{1,0:T(8,128)}, f32[1024,256]{1,0:T(8,128)}) custom-call(f32[512,1024]{1,0:T(8,128)} %trail.3, f32[64,8,128]{2,1,0:T(8,128)} %bitcast.2, f32[32,8,256]{2,1,0:T(8,128)} %bitcast.3), custom_call_target="tpu_custom_call" | custom-call | tf_op jit(solution)/shard_map/step/pallas_call | solution.py:501
  85.0 5.2 %update.1 = (f32[512,1024]{1,0:T(8,128)}, f32[512,128]{1,0:T(8,128)}, f32[512,128]{1,0:T(8,128)}) custom-call(f32[512,1024]{1,0:T(8,128)} %trail.3, f32[512,256]{1,0:T(8,128)} %get-tuple-element.7.l1r, f32[512,256]{1,0:T(8,128)} %get-tuple-element.8.l2r, f32[1024,256]{1,0:T(8,128)} %get-tuple-element.9.l1x, f32[1024,256]{1,0:T(8,128)} %get-tuple-element.10.l2x), custom_call_target="tpu_custom_call" | custom-call | tf_op jit(solution)/shard_map/update/pallas_call | solution.py:520

commit v5 on v4

--- a/solution.py
+++ b/solution.py
@@ -200,64 +200,73 @@
     r_z = new(21)
     for o in ORDER_Z:
         send(diag.at[row, :, half], zq.at[0, o - 1], r_z + o - 1, zdev(o))
+    source = (c == 0) & (z == 0)
+    xh, xp = lax.div(x, 2), lax.rem(x, 2)
+    jy, qy = lax.rem(y, 2), lax.div(y, 2)
+    mine = 2 * jy + xh
+    r_ct = new()
+    for t in range(2):
+        home = (row, xp, qy + 4 * t)
+        here = (xp == 0) & (qy + 4 * t == 0)
+        tile_t = trail.at[256 * t : 256 * (t + 1), 0:256]
+        send(tile_t, cx.at[mine], r_ct, home, source & jnp.logical_not(here))
+        if t == 0:
+            own_ct = lambda: pltpu.make_async_copy(trail.at[0:256, 0:256], cx.at[mine], loc.at[2])
+            when(source & here, lambda: own_ct().start())
     r_p0 = new()
     send_all([(panel.at[i], part, r_p0, (i, c, z)) for i in range(NX * NY - 1, 0, -1)], origin)
     r_c0 = new()
     halves = [(i, 128 * h, h) for i in range(NX * NY - 1, -1, -1) for h in range(2) if i or h]
-    send_all([(trail.at[8 * i : 8 * i + 8, w : w + 128], q.at[2, i, :, w : w + 128], r_c0, (i, h, 0)) for i, w, h in halves],
+    send_all([(trail.at[8 * i : 8 * i + 8, w : w + 128], q.at[2, i // NX, i % NX, :, w : w + 128], r_c0, (i, h, 0)) for i, w, h in halves],
              corner)
-    own_c0 = lambda: pltpu.make_async_copy(trail.at[0:8, 0:128], q.at[2, 0, :, 0:128], loc.at[1])
+    own_c0 = lambda: pltpu.make_async_copy(trail.at[0:8, 0:128], q.at[2, 0, 0, :, 0:128], loc.at[1])
     when(corner, lambda: own_c0().start())
 
-    source = (c == 0) & (z == 0)
-    xh, xp = lax.div(x, 2), lax.rem(x, 2)
-    jy, qy = lax.rem(y, 2), lax.div(y, 2)
-    mine = 2 * jy + xh
     r_qx, r_qy, r_qc = new(9), new(21), new(3)
-    from_x = lambda o: y * NX + lax.rem(x + NX - o, NX)
+    from_x = lambda o: lax.rem(x + NX - o, NX)
     from_y = lambda o: lax.rem(y + NY - o, NY)
 
+    def y_gather(a):
+        piece = q.at[a, y, x, :, half]
+        for o in (4, 3, 5, 2, 6, 1, 7):
+            send(piece, piece, r_qy + 7 * a + o - 1, ydev(o))
+
     def x_gather(a):
-        piece = q.at[a, row, :, half]
+        for o in range(1, NY):
+            recv(q.at[a, from_y(o), x, :, half], r_qy + 7 * a + o - 1)
+        piece = q.at[a, :, x, :, half]
         for o in (2, 1, 3):
             send(piece, piece, r_qx + 3 * a + o - 1, xdev(o))
 
-    def y_gather(a):
+    def core_gather(a):
         for o in range(1, NX):
-            recv(q.at[a, from_x(o), :, half], r_qx + 3 * a + o - 1)
-        piece = q.at[a, pl.ds(y * NX, NX), :, half]
-        for o in (4, 3, 5, 2, 6, 1, 7):
-            send(piece, piece, r_qy + 7 * a + o - 1, ydev(o))
-
-    def core_gather(a):
-        for o in range(1, NY):
-            recv(q.at[a, pl.ds(from_y(o) * NX, NX), :, half], r_qy + 7 * a + o - 1)
-        send(q.at[a, :, :, half], q.at[a, :, :, half], r_qc + a, other)
+            recv(q.at[a, :, from_x(o), :, half], r_qx + 3 * a + o - 1)
+        send(q.at[a, :, :, :, half], q.at[a, :, :, :, half], r_qc + a, other)
 
     def core_wait(a):
-        recv(q.at[a, :, :, half], r_qc + a)
+        recv(q.at[a, :, :, :, half], r_qc + a)
 
     def z_sum(a, own):
         total = own
         for o in range(1, NZ):
             recv(zq.at[a, o - 1], r_z + 7 * a + o - 1)
             total = total + zq[a, o - 1]
-        q[a, row, :, half] = total
+        q[a, y, x, :, half] = total
 
     holder = xp == c
     middle = xp != c
     p = lax.rem(y - 2 * lax.rem(z, 4) + NY, NY)
     rows_ch = 256 // NCH
     bufs = (px, cx)
-    near, mid_far, far = in_set(p, (0, 1, 2, 7)), in_set(p, (3, 6)), in_set(p, (4, 5))
+    classes = [in_set(p, (0, 1)), in_set(p, (2, 7)), in_set(p, (3, 6)), in_set(p, (4, 5))]
     away = jnp.where(in_set(p, (1, 2, 3)), 1, -1)
     side = (lax.div(lax.rem(x + NX - 1, NX), 2), lax.div(lax.rem(x + 1, NX), 2))
     r_y = new(4 * NCH)
     r_x = new(8 * NCH)
     root = holder & (jy == p)
-    hold_class = [holder & near, holder & mid_far, holder & far]
-    hold_near = [holder & near & (p != j) for j in range(2)]
-    mid_class = [middle & near, middle & mid_far, middle & far]
+    hold_class = [holder & k for k in classes]
+    hold_first = [holder & (p == 1 - j) for j in range(2)]
+    mid_class = [middle & k for k in classes]
 
     def at_y(a, ch, j):
         return r_y + (a * NCH + ch) * 2 + j
@@ -272,7 +281,7 @@
         items = []
         for ch in range(NCH):
             own = piece_of(a, ch, mine)
-            items += [(own, own, at_y(a, ch, jy), ydev(d)) for d in (1, -1)]
+            items += [(own, own, at_y(a, ch, jy), ydev(d)) for d in (1, -1, jnp.where(jy == 0, 2, -2))]
             items += [(own, own, at_x(a, ch, jy, s), xdev(1 - 2 * s)) for s in range(2)]
         send_all(items, root)
 
@@ -280,17 +289,17 @@
         def one(ch, j, cond):
             own = lambda: piece_of(a, ch, 2 * j + xh)
             recv(own(), at_y(a, ch, j))
-            items = [lambda: (own(), own(), at_y(a, ch, j), ydev(away))] if k < 2 else []
+            items = [lambda: (own(), own(), at_y(a, ch, j), ydev(away))] if 0 < k < 3 else []
             items += [lambda s=s: (own(), own(), at_x(a, ch, j, s), xdev(1 - 2 * s)) for s in range(2)]
             send_all(items, cond, True)
 
         if k == 0:
             for j in range(2):
 
-                @pl.when(hold_near[j])
+                @pl.when(hold_first[j])
                 def _(j=j):
                     for ch in chs:
-                        one(ch, j, hold_near[j])
+                        one(ch, j, hold_first[j])
         else:
 
             @pl.when(hold_class[k])
@@ -320,7 +329,7 @@
 
     both = tuple(range(NCH))
     z_sum(0, diag[row, :, half])
-    x_gather(0)
+    y_gather(0)
 
     @pl.when(origin)
     def _():
@@ -330,20 +339,11 @@
     for o in ORDER_Z:
         send(part, zq.at[1, o - 1], r_z + 7 + o - 1, zdev(o))
     when(corner, lambda: own_c0().wait())
-    slice_c0 = q.at[2, row, :, half]
+    slice_c0 = q.at[2, y, x, :, half]
     recv(slice_c0, r_c0, (z == 0) & jnp.logical_not(corner))
     r_cz = new()
     send_all([(slice_c0, slice_c0, r_cz, zdev(o)) for o in ORDER_Z], z == 0)
 
-    r_ct = new()
-    for t in range(2):
-        home = (row, xp, qy + 4 * t)
-        here = (xp == 0) & (qy + 4 * t == 0)
-        tile_t = trail.at[256 * t : 256 * (t + 1), 0:256]
-        send(tile_t, cx.at[mine], r_ct, home, source & jnp.logical_not(here))
-        if t == 0:
-            own_ct = lambda: pltpu.make_async_copy(trail.at[0:256, 0:256], cx.at[mine], loc.at[2])
-            when(source & here, lambda: own_ct().start())
     r_rs = new(7)
     for o in ORDER_Z:
         to = lax.rem(z + o, NZ)
@@ -355,14 +355,15 @@
     own_cs = lambda: pltpu.make_async_copy(trail.at[0:64, 0:128], rr.at[1, 0, :, 0:128], loc.at[3])
     when(source, lambda: own_cs().start())
 
-    y_gather(0)
+    here = source & (xp == 0) & (qy == 0)
+    when(here, lambda: own_ct().wait())
+    recv(cx.at[mine], r_ct, root & jnp.logical_not(here))
+    tile_source(1)
     z_sum(1, part[...])
-    x_gather(1)
+    y_gather(1)
     recv(slice_c0, r_cz, z != 0)
-    x_gather(2)
-    y_gather(1)
     y_gather(2)
-    core_gather(0)
+    x_gather(0)
     z4, zt = lax.rem(z, 4), lax.div(z, 4)
     r_pt = new(8)
     r_rp, r_rm, r_rc = new(4), new(3), new()
@@ -378,16 +379,7 @@
         if s < 3:
             send(ring_piece(s), ring_piece(s), r_rm + s, zdev(-1))
 
-    core_wait(0)
-
-    s_ref[:, :256] = q[0].reshape(256, 256)
-    chol_start(s_ref)
-    chol_steps(s_ref, y_ref, 0, 2)
-    here = source & (xp == 0) & (qy == 0)
-    when(here, lambda: own_ct().wait())
-    recv(cx.at[mine], r_ct, root & jnp.logical_not(here))
-    tile_source(1)
-
+    core_gather(0)
     total = panel[pl.ds(8 * z, 8)].reshape(64, 128)
     for o in range(1, NZ):
         recv(rs_p.at[o - 1], r_rs + o - 1)
@@ -406,11 +398,15 @@
     recv(rr.at[1, z, :, half], r_cs, jnp.logical_not(source))
     send(ring_piece(0), ring_piece(0), r_rp, zdev(1))
     send(ring_piece(0), ring_piece(0), r_rm, zdev(-1))
-    chol_steps(s_ref, y_ref, 2, 4)
     hop(1, both, 0)
-    core_gather(1)
-    core_gather(2)
-
+    x_gather(1)
+    x_gather(2)
+    core_wait(0)
+
+    s_ref[:, :256] = q[0].reshape(256, 256)
+    hop(1, both, 1)
+    chol_start(s_ref)
+    chol_steps(s_ref, y_ref, 0, 2)
     @pl.when(root)
     def _():
         for i in range(4):
@@ -419,13 +415,19 @@
                 recv(px.at[mine, 64 * i : 64 * (i + 1), 128 * h : 128 * (h + 1)], r_pt + 2 * i + h, jnp.logical_not(same))
 
     tile_source(0)
+    chol_steps(s_ref, y_ref, 2, 4)
+    ring(1)
+    core_gather(1)
+    core_gather(2)
     chol_steps(s_ref, y_ref, 4, 6)
-    hop(1, both, 1)
-    hop(0, (0,), 0)
-    ring(1)
+    hop(1, (0,), 2)
+    pass_x(1, both, 0)
+    hop(0, both, 0)
     chol_steps(s_ref, y_ref, 6, 8)
-    hop(0, both[1:], 0)
-    pass_x(1, both, 0)
+    hop(1, both[1:], 2)
+    hop(0, (0,), 1)
+    pass_x(1, both, 1)
+    ring(2)
     core_wait(1)
     core_wait(2)
     inv1 = y_ref[:, 256:]
@@ -433,30 +435,30 @@
     s_ref[:, :256] = q[2].reshape(256, 256) - mul_nt6(lead, lead)
     inv1_r = wide_right(inv1)
     lead_r = wide_right(lead)
-    hop(0, (0,), 1)
-    ring(2)
+    hop(0, both[1:], 1)
 
     chol_start(s_ref)
     chol_steps(s_ref, y_ref, 0, 2)
-    hop(0, both[1:], 1)
-    hop(1, both, 2)
-    pass_x(1, both, 1)
+    hop(0, (0,), 2)
+    hop(1, both, 3)
     pass_x(0, (0,), 0)
     ring(3)
     chol_steps(s_ref, y_ref, 2, 4)
-    hop(0, (0,), 2)
+    hop(0, both[1:], 2)
     pass_x(0, both[1:], 0)
-    pass_x(0, (0,), 1)
+    pass_x(1, both, 2)
     ring(4)
     send(rr.at[:, :, :, half], rr.at[:, :, :, half], r_rc, other)
     chol_steps(s_ref, y_ref, 4, 6)
-    hop(0, both[1:], 2)
-    pass_x(1, both, 2)
-    pass_x(0, both[1:], 1)
+    hop(0, (0,), 3)
+    pass_x(0, both, 1)
+    pass_x(1, both, 3)
     chol_steps(s_ref, y_ref, 6, 8)
+    hop(0, both[1:], 3)
+    pass_x(0, both, 2)
     tile_last(1)
     recv(rr.at[:, :, :, half], r_rc)
-    pass_x(0, both, 2)
+    pass_x(0, both, 3)
     inv2_r = wide_right(y_ref[:, 256:])
 
     l1 = wide_mul(rr[0].reshape(512, 256), inv1_r)
@@ -504,7 +506,7 @@
         in_specs=[pl.BlockSpec(memory_space=pl.ANY), vmem, vmem],
         out_specs=[vmem] * 4,
         scratch_shapes=[
-            pltpu.VMEM((3, 32, 8, 256), f32), pltpu.VMEM((2, 7, 8, 128), f32), pltpu.VMEM((8, 128), f32),
+            pltpu.VMEM((3, NY, NX, 8, 256), f32), pltpu.VMEM((2, 7, 8, 128), f32), pltpu.VMEM((8, 128), f32),
             pltpu.VMEM((7, 8, 8, 128), f32), pltpu.VMEM((2, 8, 64, 256), f32),
             pltpu.VMEM((4, 256, 256), f32), pltpu.VMEM((4, 256, 256), f32),
             pltpu.VMEM((256, 512), f32), pltpu.VMEM((256, 512), f32),

time: 90.4 us -> 79.3 us (0.88)
  the two profiles are of different devices: /device:TPU:136 before, /device:TPU:32 now
where the time goes in v5:
time: 79.3 us; the launch traced here: 79.1 us
  Pallas kernels  78.5 us (99%)
    pallas_call x1, Pallas kernels, on_device(): pl.pallas_call(step_kernel, out_shape=(shape(512, 256), shape(512, 256),...  73.3 us
    pallas_call x1, Pallas kernels, on_device(): pl.pallas_call(update_kernel, grid=(2,), out_shape=(shape(512, 1024), sha...  5.23 us

profile of v5, /device:TPU:32, one launch (start us, length us, event | category | flops | bytes accessed | tf_op | source)
XLA Modules:
  0.0 79.1 jit_solution(17623226204191374561)
XLA Ops:
  0.6 73.3 %step.1 = (f32[512,256]{1,0:T(8,128)}, f32[512,256]{1,0:T(8,128)}, f32[1024,256]{1,0:T(8,128)}, f32[1024,256]{1,0:T(8,128)}) custom-call(f32[512,1024]{1,0:T(8,128)} %trail.3, f32[64,8,128]{2,1,0:T(8,128)} %bitcast.2, f32[32,8,256]{2,1,0:T(8,128)} %bitcast.3), custom_call_target="tpu_custom_call" | custom-call | tf_op jit(solution)/shard_map/step/pallas_call | solution.py:503
  73.9 5.2 %update.1 = (f32[512,1024]{1,0:T(8,128)}, f32[512,128]{1,0:T(8,128)}, f32[512,128]{1,0:T(8,128)}) custom-call(f32[512,1024]{1,0:T(8,128)} %trail.3, f32[512,256]{1,0:T(8,128)} %get-tuple-element.7.l1r, f32[512,256]{1,0:T(8,128)} %get-tuple-element.8.l2r, f32[1024,256]{1,0:T(8,128)} %get-tuple-element.9.l1x, f32[1024,256]{1,0:T(8,128)} %get-tuple-element.10.l2x), custom_call_target="tpu_custom_call" | custom-call | tf_op jit(solution)/shard_map/update/pallas_call | solution.py:522

commit v6 on v5

--- a/solution.py
+++ b/solution.py
@@ -400,11 +400,11 @@
     send(ring_piece(0), ring_piece(0), r_rm, zdev(-1))
     hop(1, both, 0)
     x_gather(1)
+    hop(1, both, 1)
     x_gather(2)
     core_wait(0)
 
     s_ref[:, :256] = q[0].reshape(256, 256)
-    hop(1, both, 1)
     chol_start(s_ref)
     chol_steps(s_ref, y_ref, 0, 2)
     @pl.when(root)
@@ -416,16 +416,17 @@
 
     tile_source(0)
     chol_steps(s_ref, y_ref, 2, 4)
+    hop(1, (0,), 2)
     ring(1)
     core_gather(1)
     core_gather(2)
     chol_steps(s_ref, y_ref, 4, 6)
-    hop(1, (0,), 2)
+    hop(1, both[1:], 2)
     pass_x(1, both, 0)
     hop(0, both, 0)
     chol_steps(s_ref, y_ref, 6, 8)
-    hop(1, both[1:], 2)
     hop(0, (0,), 1)
+    hop(1, (0,), 3)
     pass_x(1, both, 1)
     ring(2)
     core_wait(1)
@@ -440,30 +441,31 @@
     chol_start(s_ref)
     chol_steps(s_ref, y_ref, 0, 2)
     hop(0, (0,), 2)
-    hop(1, both, 3)
+    hop(1, both[1:], 3)
     pass_x(0, (0,), 0)
     ring(3)
     chol_steps(s_ref, y_ref, 2, 4)
     hop(0, both[1:], 2)
     pass_x(0, both[1:], 0)
     pass_x(1, both, 2)
+    pass_x(1, (0,), 3)
     ring(4)
     send(rr.at[:, :, :, half], rr.at[:, :, :, half], r_rc, other)
     chol_steps(s_ref, y_ref, 4, 6)
     hop(0, (0,), 3)
     pass_x(0, both, 1)
-    pass_x(1, both, 3)
+    pass_x(1, both[1:], 3)
     chol_steps(s_ref, y_ref, 6, 8)
     hop(0, both[1:], 3)
     pass_x(0, both, 2)
-    tile_last(1)
     recv(rr.at[:, :, :, half], r_rc)
-    pass_x(0, both, 3)
     inv2_r = wide_right(y_ref[:, 256:])
 
     l1 = wide_mul(rr[0].reshape(512, 256), inv1_r)
     l1r[...] = l1
     l2r[...] = wide_mul(rr[1].reshape(512, 256) - wide_mul(l1, lead_r), inv2_r)
+    pass_x(0, both, 3)
+    tile_last(1)
     tile_last(0)
     l1 = wide_mul(px[...].reshape(1024, 256), inv1_r)
     l1x[...] = l1

time: 79.3 us -> 83 us (1.047)
  Pallas kernels: 78.5 us -> 82.2 us
    pallas_call x1, Pallas kernels: 73.3 us -> 77 us  [on_device(): pl.pallas_call(step_kernel, out_shape=(shape(512, 256), shape(512, 256),...]
where the time goes in v6:
time: 83 us; the launch traced here: 82.9 us
  Pallas kernels  82.2 us (99%)
    pallas_call x1, Pallas kernels, on_device(): pl.pallas_call(step_kernel, out_shape=(shape(512, 256), shape(512, 256),...  77 us
    pallas_call x1, Pallas kernels, on_device(): pl.pallas_call(update_kernel, grid=(2,), out_shape=(shape(512, 1024), sha...  5.24 us

profile of v6, /device:TPU:32, one launch (start us, length us, event | category | flops | bytes accessed | tf_op | source)
XLA Modules:
  0.0 82.9 jit_solution(1027167102891889973)
XLA Ops:
  0.6 77.0 %step.1 = (f32[512,256]{1,0:T(8,128)}, f32[512,256]{1,0:T(8,128)}, f32[1024,256]{1,0:T(8,128)}, f32[1024,256]{1,0:T(8,128)}) custom-call(f32[512,1024]{1,0:T(8,128)} %trail.3, f32[64,8,128]{2,1,0:T(8,128)} %bitcast.2, f32[32,8,256]{2,1,0:T(8,128)} %bitcast.3), custom_call_target="tpu_custom_call" | custom-call | tf_op jit(solution)/shard_map/step/pallas_call | solution.py:505
  77.6 5.2 %update.1 = (f32[512,1024]{1,0:T(8,128)}, f32[512,128]{1,0:T(8,128)}, f32[512,128]{1,0:T(8,128)}) custom-call(f32[512,1024]{1,0:T(8,128)} %trail.3, f32[512,256]{1,0:T(8,128)} %get-tuple-element.7.l1r, f32[512,256]{1,0:T(8,128)} %get-tuple-element.8.l2r, f32[1024,256]{1,0:T(8,128)} %get-tuple-element.9.l1x, f32[1024,256]{1,0:T(8,128)} %get-tuple-element.10.l2x), custom_call_target="tpu_custom_call" | custom-call | tf_op jit(solution)/shard_map/update/pallas_call | solution.py:524
